TPU v7x, 32 devices: a whole 2x2x4 slice. The times are simulated.
32 devices in a mesh: blk: 16 (over z, y, x), grp: 2 (over core).
Axes of the slice: x: 2, y: 2, z: 4, core: 2. Of those that a mesh axis runs over, the one named last changes fastest.
Arguments:
- text: bfloat16 [16, 384, 1024], P('blk', 'grp'), may hold values from -64 to 64
- image: bfloat16 [16, 384, 1024], P('blk', 'grp'), may hold values from -64 to 64
- pair_index: int32 [16, 384], P('blk', 'grp'), may hold values from 0 to 383, each once within a row
Outputs:
- grad_text: float32 [16, 384, 1024], P('blk', 'grp')
- grad_image: float32 [16, 384, 1024], P('blk', 'grp')
- loss: float32 [], replicated
Inputs may be any that keep to these rules, and one draw needn't show every extreme that they name: Every sub-batch's row of pair_index names each of 0 to 383 once.
All inputs are finite; a program needn't handle non-finite values.
Results may differ from a plain program's by a relative error of at most 0.0024.
Values may be sent and summed in bfloat16 or wider, within the bound.
No kernel may reach another device: no remote copies, remote signals or barrier semaphores. Data moves between devices by JAX's collectives and lax.ppermute only.
A program may use at most 64 MiB of HBM per device.

v0:
```python
import jax
import jax.numpy as jnp
from jax import lax
from jax.sharding import PartitionSpec as P

score_scale = 0.125


def merged(value, axis, join):
    pieces = jax.tree.map(lambda part: lax.all_gather(part, axis), value)
    head = jax.tree.map(lambda part: part[0], pieces)
    tail = jax.tree.map(lambda part: part[1:], pieces)
    so_far, _ = lax.scan(lambda so_far, piece: (join(so_far, piece), None), head, tail)
    return so_far


def join_stats(left, right):
    top = jnp.maximum(left[0], right[0])
    return (top, left[1] * jnp.exp(left[0] - top) + right[1] * jnp.exp(right[0] - top))


def local(text, image, pair_index):
    local_text = text[0]
    own_image = image[0]
    pairs = pair_index[0]
    rows = local_text.shape[0]
    total = rows * lax.axis_size("grp")
    offset = lax.axis_index("grp") * rows

    def scores_of(block):
        return (
            jnp.einsum("rd,nd->rn", local_text, block, preferred_element_type=jnp.float32)
            * score_scale
        )

    def hits_of(count):
        ids = jnp.arange(count, dtype=jnp.int32)
        return pairs[:, None] == ids[None, :]

    start_carry = (
        jnp.full((rows,), -1e30, jnp.float32),
        jnp.zeros((rows,), jnp.float32),
        jnp.zeros((total,), jnp.float32),
        jnp.zeros((total,), jnp.float32),
        jnp.zeros((rows,), jnp.float32),
    )
    block = lax.all_gather(image, "grp", axis=1, tiled=True)[0]
    count = block.shape[0]
    scores = scores_of(block)
    row_top = jnp.maximum(start_carry[0], jnp.max(scores, axis=1))
    row_total = jnp.sum(jnp.exp(scores - row_top[:, None]), axis=1)
    col_top = jnp.max(scores, axis=0)
    col_total = jnp.sum(jnp.exp(scores - col_top[None, :]), axis=0)
    col_tops = col_top
    col_totals = col_total
    positive = jnp.sum(jnp.where(hits_of(count), scores, 0.0), axis=1)
    result = (row_top, row_total, col_tops, col_totals, positive)
    carried = result
    row_lse = carried[0] + jnp.log(carried[1])
    positive = carried[4]
    col_top, col_total = merged((carried[2], carried[3]), "grp", join_stats)
    col_lse = col_top + jnp.log(col_total)
    block = lax.all_gather(image, "grp", axis=1, tiled=True)[0]
    count = block.shape[0]
    scores = scores_of(block)
    weight = (
        jnp.exp(scores - row_lse[:, None])
        + jnp.exp(scores - col_lse[None, :])
        - 2.0 * hits_of(count).astype(jnp.float32)
    ).astype(jnp.bfloat16)
    result = (jnp.dot(weight, block, preferred_element_type=jnp.float32),)
    grad_text = result[0] * (score_scale * 0.5)
    all_lse, pair_values = (
        lax.all_gather(row_lse, "grp", axis=0, tiled=True),
        lax.all_gather(pairs.astype(jnp.float32), "grp", axis=0, tiled=True),
    )
    all_pairs = pair_values.astype(jnp.int32)
    own_ids = offset + jnp.arange(rows, dtype=jnp.int32)
    own_col = lax.dynamic_slice_in_dim(col_lse, offset, rows, 0)
    piece = lax.all_gather(local_text, "grp", axis=0, tiled=True)
    count = piece.shape[0]
    flipped = (
        jnp.einsum("nd,kd->nk", own_image, piece, preferred_element_type=jnp.float32) * score_scale
    )
    hit_back = (all_pairs[None, :] == own_ids[:, None]).astype(jnp.float32)
    weight_back = (
        jnp.exp(flipped - all_lse[None, :]) + jnp.exp(flipped - own_col[:, None]) - 2.0 * hit_back
    ).astype(jnp.bfloat16)
    summed = jnp.dot(weight_back, piece, preferred_element_type=jnp.float32)
    grad_image = summed * (score_scale * 0.5)
    own_lse = lax.dynamic_slice_in_dim(col_lse, offset, rows, 0)
    partial_sum = jnp.sum(row_lse - 2.0 * positive) + jnp.sum(own_lse)
    loss = lax.psum(partial_sum, ("blk", "grp")) / (2.0 * total * lax.axis_size("blk"))
    return (grad_text[None], grad_image[None], loss)


def solution(mesh):
    placed = (P("blk", "grp", None), P("blk", "grp", None), P("blk", "grp"))
    return jax.shard_map(
        local,
        mesh=mesh,
        in_specs=placed,
        out_specs=(P("blk", "grp", None), P("blk", "grp", None), P()),
        check_vma=False,
    )
```

profile of v0, /device:TPU:0, one launch (start us, length us, event | category | flops | bytes accessed | tf_op | source)
XLA Modules:
  0.0 65.1 jit_solution(14665124273188576810)
XLA Ops:
  0.6 0.0 copy-start.3
  0.6 0.6 copy-done.3
  1.3 0.6 dynamic-slice
  2.5 0.0 copy-start.2
  2.6 0.7 %copy-done.2 = s32[1,192]{1,0:T(1,128)S(1)} copy-done((s32[1,192]{1,0:T(1,128)S(1)}, s32[1,192]{1,0:T(1,128)}, u32[]{:S(2)}) %copy-start.2) | copy-done | bytes 792
  3.2 0.1 convert_dynamic-update-slice_fusion
  3.3 0.0 copy-start
  3.3 2.8 %all_gather.25 = bf16[1,384,1024]{2,1,0:T(8,128)(2,1)S(1)} all-gather(bf16[1,192,1024]{2,1,0:T(8,128)(2,1)} %param.4), channel_id=1, replica_groups=mesh['blk'=16,'grp'=2] {'grp'}, dimensions={1}, use_global_device_ids=true | all-gather | bytes 1179648 | tf_op jit(solution)/shard_map/all_gather | solution.py:63
  6.1 0.0 copy-done
  6.1 0.5 fusion.43
  6.7 0.3 select_reduce_fusion
  7.0 0.6 subtract_reduce_fusion
  7.6 0.2 dynamic-update-slice
  7.8 2.5 %all-reduce.2 = (f32[384]{0:T(512)S(1)}, f32[384]{0:T(512)S(1)}) all-reduce(f32[384]{0:T(512)S(1)} %convert_dynamic-update-slice_fusion, f32[384]{0:T(512)S(1)} %dynamic-update-slice), channel_id=1, replica_groups=mesh['blk'=16,'grp'=2] {'grp'}, use_global_device_ids=true, to_apply=%add.1 | all-reduce | flops 768 | bytes 6144
  10.3 1.8 %all-gather.3 = f32[2,1,384]{2,1,0:T(1,128)S(1)} all-gather(f32[1,1,384]{2,1,0:T(1,128)S(1)} %reshape.41), channel_id=2, replica_groups=mesh['blk'=16,'grp'=2] {'grp'}, dimensions={0}, use_global_device_ids=true | all-gather | bytes 4608 | tf_op jit(solution)/shard_map/all_gather | solution.py:10
  12.1 1.8 %all-gather.4 = f32[2,1,384]{2,1,0:T(1,128)S(1)} all-gather(f32[1,1,384]{2,1,0:T(1,128)S(1)} %reshape.43), channel_id=3, replica_groups=mesh['blk'=16,'grp'=2] {'grp'}, dimensions={0}, use_global_device_ids=true | all-gather | bytes 4608 | tf_op jit(solution)/shard_map/all_gather | solution.py:10
  13.9 1.3 %fusion.1 = f32[1,192,1024]{2,1,0:T(8,128)} fusion(bf16[1,384,1024]{2,1,0:T(8,128)(2,1)S(1)} %all_gather.25, f32[192,384]{1,0:T(8,128)S(1)} %get-tuple-element.33, s32[192]{0:T(256)S(1)} %bitcast.73, f32[384]{0:T(512)S(1)} %fusion.37, f32[192]{0:T(256)S(1)} %get-tuple-element.32), kind=kOutput, calls=%fused_computation.3 | convolution fusion | flops 151707648 | bytes 1870848 | tf_op jit(solution)/shard_map/dot_general | solution.py:71
  15.3 0.7 %fusion.44 = (f32[]{:T(128)}, f32[192]{0:T(256)S(1)}) fusion(f32[384]{0:T(512)S(1)} %log_add_fusion, s32[]{:T(128)S(6)} %select_n.8), kind=kLoop, calls=%fused_computation.61 | loop fusion | flops 191 | bytes 1544 | tf_op jit(solution)/shard_map/reduce_sum | solution.py:92
  17.3 41.8 %psum.7 = f32[]{:T(128)} all-reduce(f32[]{:T(128)S(6)} %add.57), channel_id=1, replica_groups=mesh['blk'=16,'grp'=2] {'blk','grp'}, use_global_device_ids=true, to_apply=%region_7.8 | all-reduce | flops 1 | bytes 8 | tf_op jit(solution)/shard_map/psum | solution.py:93
  59.8 0.0 copy-start.1
  59.8 2.5 %all-gather.2 = bf16[1,384,1024]{2,1,0:T(8,128)(2,1)S(1)} all-gather(bf16[1,192,1024]{2,1,0:T(8,128)(2,1)S(1)} %copy-done), channel_id=4, replica_groups=mesh['blk'=16,'grp'=2] {'grp'}, dimensions={1}, use_global_device_ids=true | all-gather | bytes 1179648 | tf_op jit(solution)/shard_map/all_gather | solution.py:80
  62.3 0.0 copy-done.1
  62.3 1.7 %fusion = f32[1,192,1024]{2,1,0:T(8,128)} fusion(bf16[1,384,1024]{2,1,0:T(8,128)(2,1)S(1)} %all-gather.2, bf16[1,192,1024]{2,1,0:T(8,128)(2,1)S(1)} %copy-done.1, s32[384]{0:T(512)S(1)} %convert_element_type.16, f32[192]{0:T(256)S(1)} %get-tuple-element.30, f32[384]{0:T(512)S(1)} %get-tuple-element.28, s32[192]{0:T(256)S(1)} %iota_add_fusion), kind=kOutput, calls=%fused_computation.1 | convolution fusion | flops 302776320 | bytes 1970688 | tf_op jit(solution)/shard_map/dot_general | solution.py:89
  (11 shorter events, 0.1 us)
Async XLA Ops:
  0.6 0.7 %copy-start.3 = (u32[32]{0:T(128)S(1)}, u32[32]{0:T(128)}, u32[]{:S(2)}) copy-start(u32[32]{0:T(128)} %constant.40) | copy-start | bytes 388
  2.5 0.7 %copy-start.2 = (s32[1,192]{1,0:T(1,128)S(1)}, s32[1,192]{1,0:T(1,128)}, u32[]{:S(2)}) copy-start(s32[1,192]{1,0:T(1,128)} %param.5) | copy-start | bytes 2308
  3.3 2.8 %copy-start = (bf16[1,192,1024]{2,1,0:T(8,128)(2,1)S(1)}, bf16[1,192,1024]{2,1,0:T(8,128)(2,1)}, u32[]{:S(2)}) copy-start(bf16[1,192,1024]{2,1,0:T(8,128)(2,1)} %param.3) | copy-start | bytes 1179652
  59.8 2.5 %copy-start.1 = (bf16[1,192,1024]{2,1,0:T(8,128)(2,1)S(1)}, bf16[1,192,1024]{2,1,0:T(8,128)(2,1)}, u32[]{:S(2)}) copy-start(bf16[1,192,1024]{2,1,0:T(8,128)(2,1)} %param.4) | copy-start | bytes 1179652
where the time goes:
time: 65.5 us; the launch traced here: 65.1 us
  blocking collectives  53.3 us (81%)
  between operations  4.44 us (7%)
  matrix products  3.55 us (5%)
  local copies, waits for them, and re-layouts  2.14 us (3%)
  other arithmetic  1.7 us (3%)
    psum x1, blocking collectives, local(): lax.psum(partial_sum, ('blk', 'grp')) / (2.0 * total * lax.axis_size('blk'))  41.8 us
    all_gather x2, blocking collectives, merged(): pieces = jax.tree.map(lambda part: lax.all_gather(part, axis), value)  3.64 us
    all_gather x1, blocking collectives, local(): block = lax.all_gather(image, 'grp', axis=1, tiled=True)[0]  2.82 us
    all_gather x1, blocking collectives, local(): piece = lax.all_gather(local_text, 'grp', axis=0, tiled=True)  2.5 us
    unnamed x1, blocking collectives  2.49 us
    unnamed x14, local copies, waits for them, and re-layouts  2.1 us
    dot_general x1, matrix products, local(): summed = jnp.dot(weight_back, piece, preferred_element_type=jnp.float32)  1.69 us
    dot_general x1, matrix products, local(): result = (jnp.dot(weight, block, preferred_element_type=jnp.float32),)  1.33 us

commit v1 on v0

v1 whole, which is shorter than its diff:
```python
import functools

import jax
import jax.numpy as jnp
from jax import lax
from jax.experimental import pallas as pl
from jax.experimental.pallas import tpu as pltpu
from jax.sharding import PartitionSpec as P

score_scale = 0.125
BOTH = ("blk", "grp")


def in_order(me, count, pieces, body):
    for member in range(count):

        @pl.when(me == member)
        def _():
            body([pieces[(owner - member) % count] for owner in range(count)])


def joined(refs):
    return jnp.concatenate([ref[...] for ref in refs], axis=0)


def column_of(row):
    n = row.shape[1]
    eye = lax.broadcasted_iota(jnp.int32, (n, n), 0) == lax.broadcasted_iota(jnp.int32, (n, n), 1)
    spread = jnp.where(eye, jnp.broadcast_to(row, (n, n)), 0.0)
    return jnp.sum(spread, axis=1, keepdims=True)


def stats_kernel(count, *refs):
    texts, images, pairs = refs[:count], refs[count : 2 * count], refs[2 * count : 3 * count]
    scores_ref, row_ref, col_ref, pair_ref, part_ref = refs[3 * count :]
    me = lax.axis_index("grp")
    rows = pairs[0].shape[1]
    total = rows * count

    for k in range(count):
        owner = lax.rem(me + k, count)
        at = pl.ds(pl.multiple_of(owner * rows, rows), rows)
        pair_ref[at, :] = column_of(pairs[k][...].astype(jnp.float32)).astype(jnp.int32)

    def score(ordered):
        scores_ref[...] = (
            lax.dot_general(
                joined([t for t, _ in ordered]),
                joined([i for _, i in ordered]),
                (((1,), (1,)), ((), ())),
                preferred_element_type=jnp.float32,
            )
            * score_scale
        )

    in_order(me, count, list(zip(texts, images)), score)
    scores = scores_ref[...]
    row_top = jnp.max(scores, axis=1, keepdims=True)
    col_top = jnp.max(scores, axis=0, keepdims=True)
    row_lse = row_top + jnp.log(jnp.sum(jnp.exp(scores - row_top), axis=1, keepdims=True))
    col_lse = col_top + jnp.log(jnp.sum(jnp.exp(scores - col_top), axis=0, keepdims=True))
    row_ref[...] = row_lse
    col_ref[...] = col_lse
    ids = lax.broadcasted_iota(jnp.int32, (total, total), 1)
    hits = jnp.where(pair_ref[...] == ids, scores, 0.0)
    positive = jnp.sum(jnp.sum(hits, axis=0, keepdims=True), axis=1, keepdims=True)
    part = (
        jnp.sum(row_lse, axis=0, keepdims=True)
        + jnp.sum(col_lse, axis=1, keepdims=True)
        - 2.0 * positive
    )
    part_ref[...] = jnp.broadcast_to(part, part_ref.shape)


def weight_of(scores, row_lse, col_lse, pairs, ids):
    hit = jnp.where(pairs == ids, 2.0, 0.0)
    return (jnp.exp(scores - row_lse) + jnp.exp(scores - col_lse) - hit).astype(jnp.bfloat16)


def text_kernel(count, *refs):
    images = refs[:count]
    scores_ref, row_ref, col_ref, pair_ref, out_ref = refs[count:]
    me = lax.axis_index("grp")
    rows = out_ref.shape[0]
    at = pl.ds(pl.multiple_of(me * rows, rows), rows)
    ids = lax.broadcasted_iota(jnp.int32, (rows, rows * count), 1)
    weight = weight_of(scores_ref[at, :], row_ref[at, :], col_ref[...], pair_ref[at, :], ids)

    def multiply(ordered):
        out_ref[...] = jnp.dot(
            weight, joined(ordered), preferred_element_type=jnp.float32
        ) * (score_scale * 0.5)

    in_order(me, count, images, multiply)


def image_kernel(count, *refs):
    texts = refs[:count]
    scores_ref, row_ref, col_ref, pair_ref, out_ref = refs[count:]
    me = lax.axis_index("grp")
    rows = out_ref.shape[0]
    for member in range(count):

        @pl.when(me == member)
        def _():
            at = slice(member * rows, (member + 1) * rows)
            ids = lax.broadcasted_iota(jnp.int32, (rows * count, rows), 1) + member * rows
            weight = weight_of(
                scores_ref[:, at], row_ref[...], col_ref[:, at], pair_ref[...], ids
            )
            ordered = [texts[(owner - member) % count] for owner in range(count)]
            out_ref[...] = lax.dot_general(
                weight,
                joined(ordered),
                (((0,), (0,)), ((), ())),
                preferred_element_type=jnp.float32,
            ) * (score_scale * 0.5)


def in_vmem(n):
    return [pl.BlockSpec(memory_space=pltpu.VMEM)] * n


def local(text, image, pair_index):
    count = lax.axis_size("grp")
    blocks = lax.axis_size("blk")
    rows, width = text.shape[1:]
    total = rows * count

    def members(value):
        steps = range(1, count)
        turned = [
            lax.ppermute(value, "grp", [(i, (i - k) % count) for i in range(count)])
            for k in steps
        ]
        return [value, *turned]

    images = members(image[0])
    texts = members(text[0])
    pairs = members(pair_index)

    scores, row_lse, col_lse, pair_column, part = pl.pallas_call(
        functools.partial(stats_kernel, count),
        out_shape=(
            jax.ShapeDtypeStruct((total, total), jnp.float32),
            jax.ShapeDtypeStruct((total, 1), jnp.float32),
            jax.ShapeDtypeStruct((1, total), jnp.float32),
            jax.ShapeDtypeStruct((total, 1), jnp.int32),
            jax.ShapeDtypeStruct((1, 128), jnp.float32),
        ),
        in_specs=in_vmem(3 * count),
        out_specs=tuple(in_vmem(5)),
    )(*texts, *images, *pairs)

    if count == 2 and blocks & (blocks - 1) == 0:
        step = 1
        while step < blocks:
            moves = [(i, i ^ (2 * step + 1)) for i in range(blocks * count)]
            part = part + lax.ppermute(part, BOTH, moves)
            step *= 2
        loss = part[0, 0]
    else:
        loss = lax.psum(part[0, 0], BOTH) / count
    loss = loss / (2.0 * total * blocks)

    stats = (scores, row_lse, col_lse, pair_column)
    like = jax.ShapeDtypeStruct((rows, width), jnp.float32)

    def grad(kernel, pieces):
        return pl.pallas_call(
            functools.partial(kernel, count),
            out_shape=like,
            in_specs=in_vmem(count + 4),
            out_specs=pl.BlockSpec(memory_space=pltpu.VMEM),
            cost_estimate=pl.CostEstimate(
                flops=2 * rows * total * width, bytes_accessed=4 * rows * width, transcendentals=0
            ),
        )(*pieces, *stats)

    grad_text = grad(text_kernel, images)
    grad_image = grad(image_kernel, texts)
    return grad_text[None], grad_image[None], loss


def solution(mesh):
    placed = (P("blk", "grp", None), P("blk", "grp", None), P("blk", "grp"))
    return jax.shard_map(
        local,
        mesh=mesh,
        in_specs=placed,
        out_specs=(P("blk", "grp", None), P("blk", "grp", None), P()),
        check_vma=False,
    )
```

time: 65.5 us -> 27.2 us (0.42)
  blocking collectives: 53.3 us -> 0 us
  starting transfers between devices: 0 us -> 9.97 us
  Pallas kernels: 0 us -> 8.87 us
  waiting for transfers between devices: 0 us -> 4.12 us
  matrix products: 3.55 us -> 0 us
  between operations: 4.44 us -> 1.83 us
  other arithmetic: 1.7 us -> 0.01 us
    psum x1 -> x0, blocking collectives: 41.8 us -> none  [local(): lax.psum(partial_sum, ('blk', 'grp')) / (2.0 * total * lax.axis_size('blk'))]
    ppermute x0 -> x7, starting transfers between devices: none -> 9.97 us  [the longest x4 8.84 us: local(): part = part + lax.ppermute(part, BOTH, moves)]
    all_gather x4 -> x0, blocking collectives: 8.96 us -> none  [the longest x2 3.64 us: merged(): pieces = jax.tree.map(lambda part: lax.all_gather(part, axis), value)]
    pallas_call x0 -> x3, Pallas kernels: none -> 8.87 us  [the longest x2 5.76 us: grad(): pl.pallas_call(functools.partial(kernel, count), out_shape=like, in_specs...]
    ppermute x0 -> x7, waiting for transfers between devices: none -> 4.12 us  [the longest x4 2.6 us: local(): part = part + lax.ppermute(part, BOTH, moves)]
    dot_general x3 -> x0, matrix products: 3.55 us -> none  [the longest x1 1.69 us: local(): summed = jnp.dot(weight_back, piece, preferred_element_type=jnp.float32)]
    unnamed x1 -> x0, blocking collectives: 2.49 us -> none
    reduce_sum x3 -> x0, other arithmetic: 1.55 us -> none  [the longest x2 1.29 us: local(): partial_sum = jnp.sum(row_lse - 2.0 * positive) + jnp.sum(own_lse)]
  transfers between devices with their start and end apart: 0 -> 7, of which waited for: 0 -> 3; matrix products, arithmetic and copies ran while one was open for 0% -> 0% of each run, Pallas kernels for 0% -> 21%
where the time goes in v1:
time: 27.2 us; the launch traced here: 27 us
  starting transfers between devices  9.97 us (37%)
  Pallas kernels  8.87 us (33%)
  waiting for transfers between devices  4.12 us (15%)
  local copies, waits for them, and re-layouts  2.17 us (8%)
  between operations  1.83 us (7%)
    ppermute x4, starting transfers between devices, local(): part = part + lax.ppermute(part, BOTH, moves)  8.84 us
    pallas_call x2, Pallas kernels, grad(): pl.pallas_call(functools.partial(kernel, count), out_shape=like, in_specs...  5.76 us
    pallas_call x1, Pallas kernels, local(): pl.pallas_call(functools.partial(stats_kernel, count), out_shape=(jax.Sha...  3.12 us
    ppermute x4, waiting for transfers between devices, local(): part = part + lax.ppermute(part, BOTH, moves)  2.6 us
    unnamed x10, local copies, waits for them, and re-layouts  2.17 us
    ppermute x3, waiting for transfers between devices, members(): lax.ppermute(value, 'grp', [(i, (i - k) % count) for i in range(count)])  1.52 us
    ppermute x3, starting transfers between devices, members(): lax.ppermute(value, 'grp', [(i, (i - k) % count) for i in range(count)])  1.13 us
  transfers between devices with their start and end apart: 7, of which 3 were waited for; matrix products, arithmetic and copies ran while one was open for 0% of the time, Pallas kernels for 21%

profile of v1, /device:TPU:0, one launch (start us, length us, event | category | flops | bytes accessed | tf_op | source)
XLA Modules:
  0.0 27.0 jit_solution(6015497303975186145)
XLA Ops:
  0.6 0.0 copy-start.2
  0.6 0.6 %collective-permute-start.1 = (bf16[192,1024]{1,0:T(8,128)(2,1)}, bf16[192,1024]{1,0:T(8,128)(2,1)S(1)}, u32[]{:S(2)}, u32[]{:S(2)}) collective-permute-start(bf16[192,1024]{1,0:T(8,128)(2,1)} %bitcast.6), channel_id=1, source_target_pairs={{0,1},{1,0},{2,3},{3,2},{4,5},{5,4},{6,7},{7,6},{8,9},{9,8},{10,11... | collective-permute-start | bytes 1179656 | tf_op jit(solution)/shard_map/ppermute | solution.py:133
  1.2 0.1 collective-permute-start
  1.3 0.0 copy-done.2
  1.3 0.5 %collective-permute-start.2 = (s32[1,192]{1,0:T(1,128)S(1)}, s32[1,192]{1,0:T(1,128)S(1)}, u32[]{:S(2)}, u32[]{:S(2)}) collective-permute-start(s32[1,192]{1,0:T(1,128)S(1)} %copy-done.2), channel_id=1, source_target_pairs={{0,1},{1,0},{2,3},{3,2},{4,5},{5,4},{6,7},{7,6},{8,9},{9,8},{10,11... | collective-permute-start | bytes 2312 | tf_op jit(solution)/shard_map/ppermute | solution.py:133
  1.8 1.5 %collective-permute-done.2.refs_5_ = s32[1,192]{1,0:T(1,128)S(1)} collective-permute-done((s32[1,192]{1,0:T(1,128)S(1)}, s32[1,192]{1,0:T(1,128)S(1)}, u32[]{:S(2)}, u32[]{:S(2)}) %collective-permute-start.2) | collective-permute-done | bytes 800 | tf_op jit(solution)/shard_map/ppermute | solution.py:133
  3.3 0.0 copy-start.3
  3.3 0.0 collective-permute-done.1.refs_1_
  3.3 0.0 copy-start.1
  3.3 0.0 collective-permute-done.refs_3_.refs_1_
  3.3 0.5 %copy-done.3 = s32[1,192]{1,0:T(1,128)} copy-done((s32[1,192]{1,0:T(1,128)}, s32[1,192]{1,0:T(1,128)S(1)}, u32[]{:S(2)}) %copy-start.3) | copy-done | bytes 792
  3.9 0.2 copy-done.1
  4.1 0.0 copy-start
  4.1 0.7 %copy-done = bf16[192,1024]{1,0:T(8,128)(2,1)} copy-done((bf16[192,1024]{1,0:T(8,128)(2,1)}, bf16[192,1024]{1,0:T(8,128)(2,1)S(1)}, u32[]{:S(2)}) %copy-start) | copy-done | bytes 393240
  4.8 3.1 %shard_map.58 = (f32[384,384]{1,0:T(8,128)}, f32[384,1]{1,0:T(8,128)}, f32[1,384]{1,0:T(1,128)}, s32[384,1]{1,0:T(8,128)}, f32[1,128]{1,0:T(1,128)}) custom-call(bf16[192,1024]{1,0:T(8,128)(2,1)} %bitcast.7, bf16[192,1024]{1,0:T(8,128)(2,1)} %copy-done.1, bf16[192,1024]{1,0:T(8,128)(2,1)} %bitcast.10, bf16[192,1024]{1,0:T(8,128)(2,1)} %copy-done, ...), custom_call_target="tpu_custom_call" | custom-call | tf_op jit(solution)/shard_map/pallas_call | solution.py:142
  7.9 0.0 copy-start.4
  7.9 0.7 %copy-done.4 = f32[1,128]{1,0:T(1,128)S(1)} copy-done((f32[1,128]{1,0:T(1,128)S(1)}, f32[1,128]{1,0:T(1,128)}, u32[]{:S(2)}) %copy-start.4) | copy-done | bytes 536
  8.6 2.6 %collective-permute-start.3 = (f32[1,128]{1,0:T(1,128)S(1)}, f32[1,128]{1,0:T(1,128)S(1)}, u32[]{:S(2)}, u32[]{:S(2)}) collective-permute-start(f32[1,128]{1,0:T(1,128)S(1)} %copy-done.4), channel_id=1, source_target_pairs={{0,3},{1,2},{2,1},{3,0},{4,7},{5,6},{6,5},{7,4},{8,11},{9,10},{10,... | collective-permute-start | bytes 1544 | tf_op jit(solution)/shard_map/ppermute | solution.py:159
  11.2 1.3 %collective-permute-done.3 = f32[1,128]{1,0:T(1,128)S(1)} collective-permute-done((f32[1,128]{1,0:T(1,128)S(1)}, f32[1,128]{1,0:T(1,128)S(1)}, u32[]{:S(2)}, u32[]{:S(2)}) %collective-permute-start.3) | collective-permute-done | bytes 544 | tf_op jit(solution)/shard_map/ppermute | solution.py:159
  12.5 1.7 %collective-permute-start.4 = (f32[1,128]{1,0:T(1,128)S(1)}, f32[1,128]{1,0:T(1,128)S(1)}, u32[]{:S(2)}, u32[]{:S(2)}) collective-permute-start(f32[1,128]{1,0:T(1,128)S(1)} %add.12), channel_id=1, source_target_pairs={{0,5},{1,4},{2,7},{3,6},{4,1},{5,0},{6,3},{7,2},{8,13},{9,12},{10,... | collective-permute-start | bytes 1544 | tf_op jit(solution)/shard_map/ppermute | solution.py:159
  14.2 1.3 %collective-permute-done.4 = f32[1,128]{1,0:T(1,128)S(1)} collective-permute-done((f32[1,128]{1,0:T(1,128)S(1)}, f32[1,128]{1,0:T(1,128)S(1)}, u32[]{:S(2)}, u32[]{:S(2)}) %collective-permute-start.4) | collective-permute-done | bytes 544 | tf_op jit(solution)/shard_map/ppermute | solution.py:159
  15.5 1.8 %collective-permute-start.5 = (f32[1,128]{1,0:T(1,128)S(1)}, f32[1,128]{1,0:T(1,128)S(1)}, u32[]{:S(2)}, u32[]{:S(2)}) collective-permute-start(f32[1,128]{1,0:T(1,128)S(1)} %add.13), channel_id=1, source_target_pairs={{0,9},{1,8},{2,11},{3,10},{4,13},{5,12},{6,15},{7,14},{8,1},{9,0},... | collective-permute-start | bytes 1544 | tf_op jit(solution)/shard_map/ppermute | solution.py:159
  17.3 2.9 %shard_map.60 = f32[192,1024]{1,0:T(8,128)} custom-call(bf16[192,1024]{1,0:T(8,128)(2,1)} %bitcast.8, bf16[192,1024]{1,0:T(8,128)(2,1)} %copy-done.1, f32[384,384]{1,0:T(8,128)} %get-tuple-element.8.refs_2_, f32[384,1]{1,0:T(8,128)} %get-tuple-element.9.refs_3_, f32[1,384]{1,0:T(1,128)} %get-tuple-element.10.refs_4_, s32[384,1]{1,0:T(8,128)} %get-tuple-element.11.refs_5_), custom_call_target="tpu_custom_call" | custom-call | flops 150994944 | bytes 786432 | tf_op jit(solution)/shard_map/pallas_call | solution.py:170
  20.2 0.0 collective-permute-done.5
  20.2 2.7 %collective-permute-start.6 = (f32[1,128]{1,0:T(1,128)S(1)}, f32[1,128]{1,0:T(1,128)S(1)}, u32[]{:S(2)}, u32[]{:S(2)}) collective-permute-start(f32[1,128]{1,0:T(1,128)S(1)} %add.14), channel_id=1, source_target_pairs={{0,17},{1,16},{2,19},{3,18},{4,21},{5,20},{6,23},{7,22},{8,25},{9,... | collective-permute-start | bytes 1544 | tf_op jit(solution)/shard_map/ppermute | solution.py:159
  22.9 2.8 %shard_map.59 = f32[192,1024]{1,0:T(8,128)} custom-call(bf16[192,1024]{1,0:T(8,128)(2,1)} %bitcast.11, bf16[192,1024]{1,0:T(8,128)(2,1)} %copy-done, f32[384,384]{1,0:T(8,128)} %get-tuple-element.8.refs_2_, f32[384,1]{1,0:T(8,128)} %get-tuple-element.9.refs_3_, f32[1,384]{1,0:T(1,128)} %get-tuple-element.10.refs_4_, s32[384,1]{1,0:T(8,128)} %get-tuple-element.11.refs_5_), custom_call_target="tpu_custom_call" | custom-call | flops 150994944 | bytes 786432 | tf_op jit(solution)/shard_map/pallas_call | solution.py:170
  25.8 0.0 collective-permute-done.6
  (4 shorter events, 0.0 us)
Async XLA Ops:
  0.6 0.7 %copy-start.2 = (s32[1,192]{1,0:T(1,128)S(1)}, s32[1,192]{1,0:T(1,128)}, u32[]{:S(2)}) copy-start(s32[1,192]{1,0:T(1,128)} %refs_4_.1) | copy-start | bytes 2308
  0.6 2.7 %collective-permute-start.1 = (bf16[192,1024]{1,0:T(8,128)(2,1)}, bf16[192,1024]{1,0:T(8,128)(2,1)S(1)}, u32[]{:S(2)}, u32[]{:S(2)}) collective-permute-start(bf16[192,1024]{1,0:T(8,128)(2,1)} %bitcast.6), channel_id=1, source_target_pairs={{0,1},{1,0},{2,3},{3,2},{4,5},{5,4},{6,7},{7,6},{8,9},{9,8},{10,11... | collective-permute-start | bytes 1179656 | tf_op jit(solution)/shard_map/ppermute | solution.py:133
  1.2 2.1 %collective-permute-start = (bf16[192,1024]{1,0:T(8,128)(2,1)}, bf16[192,1024]{1,0:T(8,128)(2,1)S(1)}, u32[]{:S(2)}, u32[]{:S(2)}) collective-permute-start(bf16[192,1024]{1,0:T(8,128)(2,1)} %bitcast.9), channel_id=1, source_target_pairs={{0,1},{1,0},{2,3},{3,2},{4,5},{5,4},{6,7},{7,6},{8,9},{9,8},{10,11... | collective-permute-start | bytes 1179656 | tf_op jit(solution)/shard_map/ppermute | solution.py:133
  1.3 2.0 %collective-permute-start.2 = (s32[1,192]{1,0:T(1,128)S(1)}, s32[1,192]{1,0:T(1,128)S(1)}, u32[]{:S(2)}, u32[]{:S(2)}) collective-permute-start(s32[1,192]{1,0:T(1,128)S(1)} %copy-done.2), channel_id=1, source_target_pairs={{0,1},{1,0},{2,3},{3,2},{4,5},{5,4},{6,7},{7,6},{8,9},{9,8},{10,11... | collective-permute-start | bytes 2312 | tf_op jit(solution)/shard_map/ppermute | solution.py:133
  3.3 0.6 %copy-start.3 = (s32[1,192]{1,0:T(1,128)}, s32[1,192]{1,0:T(1,128)S(1)}, u32[]{:S(2)}) copy-start(s32[1,192]{1,0:T(1,128)S(1)} %collective-permute-done.2.refs_5_) | copy-start | bytes 2308
  3.3 0.7 %copy-start.1 = (bf16[192,1024]{1,0:T(8,128)(2,1)}, bf16[192,1024]{1,0:T(8,128)(2,1)S(1)}, u32[]{:S(2)}) copy-start(bf16[192,1024]{1,0:T(8,128)(2,1)S(1)} %collective-permute-done.1.refs_1_) | copy-start | bytes 1179652
  4.1 0.7 %copy-start = (bf16[192,1024]{1,0:T(8,128)(2,1)}, bf16[192,1024]{1,0:T(8,128)(2,1)S(1)}, u32[]{:S(2)}) copy-start(bf16[192,1024]{1,0:T(8,128)(2,1)S(1)} %collective-permute-done.refs_3_.refs_1_) | copy-start | bytes 1179652
  7.9 0.7 %copy-start.4 = (f32[1,128]{1,0:T(1,128)S(1)}, f32[1,128]{1,0:T(1,128)}, u32[]{:S(2)}) copy-start(f32[1,128]{1,0:T(1,128)} %get-tuple-element.12) | copy-start | bytes 1540
  8.6 3.9 %collective-permute-start.3 = (f32[1,128]{1,0:T(1,128)S(1)}, f32[1,128]{1,0:T(1,128)S(1)}, u32[]{:S(2)}, u32[]{:S(2)}) collective-permute-start(f32[1,128]{1,0:T(1,128)S(1)} %copy-done.4), channel_id=1, source_target_pairs={{0,3},{1,2},{2,1},{3,0},{4,7},{5,6},{6,5},{7,4},{8,11},{9,10},{10,... | collective-permute-start | bytes 1544 | tf_op jit(solution)/shard_map/ppermute | solution.py:159
  12.5 3.0 %collective-permute-start.4 = (f32[1,128]{1,0:T(1,128)S(1)}, f32[1,128]{1,0:T(1,128)S(1)}, u32[]{:S(2)}, u32[]{:S(2)}) collective-permute-start(f32[1,128]{1,0:T(1,128)S(1)} %add.12), channel_id=1, source_target_pairs={{0,5},{1,4},{2,7},{3,6},{4,1},{5,0},{6,3},{7,2},{8,13},{9,12},{10,... | collective-permute-start | bytes 1544 | tf_op jit(solution)/shard_map/ppermute | solution.py:159
  15.5 4.7 %collective-permute-start.5 = (f32[1,128]{1,0:T(1,128)S(1)}, f32[1,128]{1,0:T(1,128)S(1)}, u32[]{:S(2)}, u32[]{:S(2)}) collective-permute-start(f32[1,128]{1,0:T(1,128)S(1)} %add.13), channel_id=1, source_target_pairs={{0,9},{1,8},{2,11},{3,10},{4,13},{5,12},{6,15},{7,14},{8,1},{9,0},... | collective-permute-start | bytes 1544 | tf_op jit(solution)/shard_map/ppermute | solution.py:159
  20.2 5.6 %collective-permute-start.6 = (f32[1,128]{1,0:T(1,128)S(1)}, f32[1,128]{1,0:T(1,128)S(1)}, u32[]{:S(2)}, u32[]{:S(2)}) collective-permute-start(f32[1,128]{1,0:T(1,128)S(1)} %add.14), channel_id=1, source_target_pairs={{0,17},{1,16},{2,19},{3,18},{4,21},{5,20},{6,23},{7,22},{8,25},{9,... | collective-permute-start | bytes 1544 | tf_op jit(solution)/shard_map/ppermute | solution.py:159

commit v2 on v0

v2 whole, which is shorter than its diff:
```python
import functools

import jax
import jax.numpy as jnp
from jax import lax
from jax.experimental import pallas as pl
from jax.experimental.pallas import tpu as pltpu
from jax.sharding import PartitionSpec as P


score_scale = 0.125
grad_scale = score_scale * 0.5
kernel_vmem = 24 << 20
BOTH = ("blk", "grp")


def column_of(row):
    n = row.shape[1]
    eye = lax.broadcasted_iota(jnp.int32, (n, n), 0) == lax.broadcasted_iota(jnp.int32, (n, n), 1)
    spread = jnp.where(eye, jnp.broadcast_to(row.astype(jnp.float32), (n, n)), 0.0)
    return jnp.sum(spread, axis=1, keepdims=True).astype(jnp.int32)


def square(text, image):
    both_last = (((1,), (1,)), ((), ()))
    return lax.dot_general(text, image, both_last, preferred_element_type=jnp.float32) * score_scale


def hit_of(count, pair_column, piece):
    rows = pair_column.shape[0]
    base = lax.rem(lax.axis_index("grp") + piece, count) * rows
    return pair_column - base == lax.broadcasted_iota(jnp.int32, (rows, rows), 1)


def own_kernel(text_hbm, image_hbm, pair_ref, text_ref, image_ref, pair_column_ref, score_ref, sems):
    loads = [
        pltpu.make_async_copy(text_hbm, text_ref, sems.at[0]),
        pltpu.make_async_copy(image_hbm, image_ref, sems.at[1]),
    ]
    for load in loads:
        load.start()
    pair_column_ref[...] = column_of(pair_ref[...])
    for load in loads:
        load.wait()
    score_ref[...] = square(text_ref[...], image_ref[...])


def stats_kernel(count, mean, *refs):
    refs = list(refs)

    def take(n):
        taken = refs[:n]
        del refs[:n]
        return taken

    texts, images, pairs = take(count), take(count), take(count - 1)
    own_score, own_pair = take(2)
    row_scores, col_scores = take(count - 1), take(count - 1)
    row_lses, col_lses, pair_columns = take(count), take(count), take(count - 1)
    (part_ref,) = take(1)
    rest = take((count - 1) ** 2)

    members = range(count)
    scores = {(0, 0): own_score}
    for k in range(1, count):
        scores[0, k] = row_scores[k - 1]
        scores[k, 0] = col_scores[k - 1]
    for a in range(1, count):
        for b in range(1, count):
            scores[a, b] = rest[(a - 1) * (count - 1) + b - 1]
    for b in members:
        for a in members:
            if a or b:
                scores[a, b][...] = square(texts[a][...], images[b][...])
    columns = [own_pair, *pair_columns]
    for k in range(1, count):
        pair_columns[k - 1][...] = column_of(pairs[k - 1][...])

    def added(values):
        return functools.reduce(jnp.add, values)

    def largest(values):
        return functools.reduce(jnp.maximum, values)

    def lse(line, axis):
        top = jnp.max(largest([s[...] for s in line]), axis=axis, keepdims=True)
        total = jnp.sum(added([jnp.exp(s[...] - top) for s in line]), axis=axis, keepdims=True)
        return top + jnp.log(total)

    for k in members:
        row_lses[k][...] = lse([scores[k, b] for b in members], 1)
        col_lses[k][...] = lse([scores[a, k] for a in members], 0)
    positive = 0.0
    for shift in members:
        positive += added(
            [
                jnp.where(
                    hit_of(count, columns[a][...], (a + shift) % count),
                    scores[a, (a + shift) % count][...],
                    0.0,
                )
                for a in members
            ]
        )
    part = (
        jnp.sum(added([r[...] for r in row_lses]), axis=0, keepdims=True)
        + jnp.sum(added([c[...] for c in col_lses]), axis=1, keepdims=True)
        - 2.0 * jnp.sum(jnp.sum(positive, axis=0, keepdims=True), axis=1, keepdims=True)
    )
    part_ref[...] = jnp.broadcast_to(part * mean, part_ref.shape)


def weight_of(score, row_lse, col_lse, hit):
    both = jnp.exp(score - row_lse) + jnp.exp(score - col_lse)
    return (both - jnp.where(hit, 2.0, 0.0)).astype(jnp.bfloat16)


def text_kernel(count, *refs):
    images, scores, cols = refs[:count], refs[count : 2 * count], refs[2 * count : 3 * count]
    row, pair, out_ref = refs[3 * count :]
    total = None
    for k in range(count):
        weight = weight_of(
            scores[k][...], row[...], cols[k][...], hit_of(count, pair[...], k)
        )
        term = jnp.dot(weight, images[k][...], preferred_element_type=jnp.float32)
        total = term if total is None else total + term
    out_ref[...] = total * grad_scale


def image_kernel(count, *refs):
    texts, scores, rows = refs[:count], refs[count : 2 * count], refs[2 * count : 3 * count]
    pairs = refs[3 * count : 4 * count]
    col, out_ref = refs[4 * count :]
    both_first = (((0,), (0,)), ((), ()))
    total = None
    for k in range(count):
        weight = weight_of(
            scores[k][...], rows[k][...], col[...], hit_of(count, pairs[k][...], 0)
        )
        term = lax.dot_general(
            weight, texts[k][...], both_first, preferred_element_type=jnp.float32
        )
        total = term if total is None else total + term
    out_ref[...] = total * grad_scale


def in_vmem(n):
    return [pl.BlockSpec(memory_space=pltpu.VMEM)] * n


def call(kernel, out_shape, args, flops, scratch=()):
    single = not isinstance(out_shape, tuple)
    return pl.pallas_call(
        kernel,
        out_shape=out_shape,
        in_specs=in_vmem(len(args)),
        out_specs=in_vmem(1)[0] if single else tuple(in_vmem(len(out_shape))),
        scratch_shapes=scratch,
        compiler_params=pltpu.CompilerParams(vmem_limit_bytes=kernel_vmem),
        cost_estimate=pl.CostEstimate(flops=flops, bytes_accessed=1, transcendentals=0),
    )(*[pltpu.with_memory_space_constraint(arg, pltpu.VMEM) for arg in args])


def local(text, image, pair_index):
    count = lax.axis_size("grp")
    blocks = lax.axis_size("blk")
    rows, width = text.shape[1:]
    total = rows * count
    dot_flops = 2 * rows * rows * width

    def others(value):
        return [
            lax.ppermute(value, "grp", [(i, (i - k) % count) for i in range(count)])
            for k in range(1, count)
        ]

    def piece(shape, dtype=jnp.float32):
        return pltpu.VMEM(shape, dtype)

    other_images = others(image[0])
    other_texts = others(text[0])
    other_pairs = others(pair_index)

    own_text, own_image, own_pair, own_score = pl.pallas_call(
        own_kernel,
        out_shape=(
            piece((rows, width), text.dtype),
            piece((rows, width), image.dtype),
            piece((rows, 1), jnp.int32),
            piece((rows, rows)),
        ),
        in_specs=[pl.BlockSpec(memory_space=pltpu.HBM)] * 2 + in_vmem(1),
        out_specs=tuple(in_vmem(4)),
        scratch_shapes=[pltpu.SemaphoreType.DMA((2,))],
        compiler_params=pltpu.CompilerParams(vmem_limit_bytes=kernel_vmem),
        cost_estimate=pl.CostEstimate(flops=20 * dot_flops, bytes_accessed=1, transcendentals=0),
    )(
        pltpu.with_memory_space_constraint(text[0], pltpu.HBM),
        pltpu.with_memory_space_constraint(image[0], pltpu.HBM),
        pltpu.with_memory_space_constraint(pair_index, pltpu.VMEM),
    )

    texts = [own_text, *other_texts]
    images = [own_image, *other_images]
    line = [piece((rows, rows))] * (count - 1)
    results = call(
        functools.partial(stats_kernel, count, 1.0 / (2.0 * total * blocks)),
        (
            *line,
            *line,
            *[piece((rows, 1))] * count,
            *[piece((1, rows))] * count,
            *[piece((rows, 1), jnp.int32)] * (count - 1),
            piece((1, 128)),
        ),
        [*texts, *images, *other_pairs, own_score, own_pair],
        dot_flops * count * count,
        [piece((rows, rows))] * (count - 1) ** 2,
    )
    results = list(results)
    row_scores = [own_score, *results[: count - 1]]
    col_scores = [own_score, *results[count - 1 : 2 * count - 2]]
    results = results[2 * count - 2 :]
    row_lses, col_lses = results[:count], results[count : 2 * count]
    pairs = [own_pair, *results[2 * count : -1]]
    part = results[-1]

    if count == 2 and blocks & (blocks - 1) == 0:
        step = 1
        while step < blocks:
            moves = [(i, i ^ (2 * step + 1)) for i in range(blocks * count)]
            part = part + lax.ppermute(part, BOTH, moves)
            step *= 2
        loss = part[0, 0]
    else:
        loss = lax.psum(part[0, 0], BOTH) / count

    like = jax.ShapeDtypeStruct((rows, width), jnp.float32)
    grad_text = call(
        functools.partial(text_kernel, count),
        like,
        [*images, *row_scores, *col_lses, row_lses[0], own_pair],
        4 * dot_flops * count,
    )
    grad_image = call(
        functools.partial(image_kernel, count),
        like,
        [*texts, *col_scores, *row_lses, *pairs, col_lses[0]],
        4 * dot_flops * count,
    )
    return grad_text[None], grad_image[None], loss


def solution(mesh):
    placed = (P("blk", "grp", None), P("blk", "grp", None), P("blk", "grp"))
    return jax.shard_map(
        local,
        mesh=mesh,
        in_specs=placed,
        out_specs=(P("blk", "grp", None), P("blk", "grp", None), P()),
        check_vma=False,
    )
```

time: 65.5 us -> 19.2 us (0.29)
  blocking collectives: 53.3 us -> 0 us
  starting transfers between devices: 0 us -> 9.87 us
  Pallas kernels: 0 us -> 5.27 us
  between operations: 4.44 us -> 0.66 us
  matrix products: 3.55 us -> 0 us
  waiting for transfers between devices: 0 us -> 2.7 us
  local copies, waits for them, and re-layouts: 2.14 us -> 0.04 us
  other arithmetic: 1.7 us -> 0.52 us
    psum x1 -> x0, blocking collectives: 41.8 us -> none  [local(): lax.psum(partial_sum, ('blk', 'grp')) / (2.0 * total * lax.axis_size('blk'))]
    ppermute x0 -> x7, starting transfers between devices: none -> 9.87 us  [the longest x4 8.74 us: local(): part = part + lax.ppermute(part, BOTH, moves)]
    all_gather x4 -> x0, blocking collectives: 8.96 us -> none  [the longest x2 3.64 us: merged(): pieces = jax.tree.map(lambda part: lax.all_gather(part, axis), value)]
    pallas_call x0 -> x4, Pallas kernels: none -> 5.27 us  [the longest x3 3.85 us: call(): pl.pallas_call(kernel, out_shape=out_shape, in_specs=in_vmem(len(args)),...]
    dot_general x3 -> x0, matrix products: 3.55 us -> none  [the longest x1 1.69 us: local(): summed = jnp.dot(weight_back, piece, preferred_element_type=jnp.float32)]
    ppermute x0 -> x7, waiting for transfers between devices: none -> 2.7 us  [the longest x4 2.6 us: local(): part = part + lax.ppermute(part, BOTH, moves)]
    unnamed x1 -> x0, blocking collectives: 2.49 us -> none
    unnamed x14 -> x2, local copies, waits for them, and re-layouts: 2.1 us -> 0.04 us
  transfers between devices with their start and end apart: 0 -> 7, of which waited for: 0 -> 3; matrix products, arithmetic and copies ran while one was open for 0% -> 0% of each run, Pallas kernels for 0% -> 22%
where the time goes in v2:
time: 19.2 us; the launch traced here: 19.1 us
  starting transfers between devices  9.87 us (51%)
  Pallas kernels  5.27 us (27%)
  waiting for transfers between devices  2.7 us (14%)
  between operations  0.66 us (3%)
  other arithmetic  0.52 us (3%)
    ppermute x4, starting transfers between devices, local(): part = part + lax.ppermute(part, BOTH, moves)  8.74 us
    pallas_call x3, Pallas kernels, call(): pl.pallas_call(kernel, out_shape=out_shape, in_specs=in_vmem(len(args)),...  3.85 us
    ppermute x4, waiting for transfers between devices, local(): part = part + lax.ppermute(part, BOTH, moves)  2.6 us
    pallas_call x1, Pallas kernels, local(): pl.pallas_call(own_kernel, out_shape=(piece((rows, width), text.dtype), p...  1.42 us
    ppermute x3, starting transfers between devices, others(): lax.ppermute(value, 'grp', [(i, (i - k) % count) for i in range(count)])  1.13 us
    add x4, other arithmetic, local(): part = part + lax.ppermute(part, BOTH, moves)  0.52 us
  transfers between devices with their start and end apart: 7, of which 3 were waited for; matrix products, arithmetic and copies ran while one was open for 0% of the time, Pallas kernels for 22%

profile of v2, /device:TPU:0, one launch (start us, length us, event | category | flops | bytes accessed | tf_op | source)
XLA Modules:
  0.0 19.1 jit_solution(143827085725803370)
XLA Ops:
  0.6 0.0 copy-start
  0.6 0.6 %collective-permute-start.1 = (bf16[192,1024]{1,0:T(8,128)(2,1)}, bf16[192,1024]{1,0:T(8,128)(2,1)S(1)}, u32[]{:S(2)}, u32[]{:S(2)}) collective-permute-start(bf16[192,1024]{1,0:T(8,128)(2,1)} %bitcast.7), channel_id=1, source_target_pairs={{0,1},{1,0},{2,3},{3,2},{4,5},{5,4},{6,7},{7,6},{8,9},{9,8},{10,11... | collective-permute-start | bytes 1179656 | tf_op jit(solution)/shard_map/ppermute | solution.py:174
  1.2 0.1 collective-permute-start
  1.3 0.0 copy-done
  1.3 0.5 %collective-permute-start.2 = (s32[1,192]{1,0:T(1,128)S(1)}, s32[1,192]{1,0:T(1,128)S(1)}, u32[]{:S(2)}, u32[]{:S(2)}) collective-permute-start(s32[1,192]{1,0:T(1,128)S(1)} %copy-done), channel_id=1, source_target_pairs={{0,1},{1,0},{2,3},{3,2},{4,5},{5,4},{6,7},{7,6},{8,9},{9,8},{10,11... | collective-permute-start | bytes 2312 | tf_op jit(solution)/shard_map/ppermute | solution.py:174
  1.8 1.4 %shard_map.58 = (bf16[192,1024]{1,0:T(8,128)(2,1)S(1)}, bf16[192,1024]{1,0:T(8,128)(2,1)S(1)}, s32[192,1]{1,0:T(8,128)S(1)}, f32[192,192]{1,0:T(8,128)S(1)}) custom-call(bf16[192,1024]{1,0:T(8,128)(2,1)} %bitcast.8, bf16[192,1024]{1,0:T(8,128)(2,1)} %bitcast.10, s32[1,192]{1,0:T(1,128)S(1)} %copy-done), custom_call_target="tpu_custom_call" | custom-call | flops 1509949440 | bytes 1 | tf_op jit(solution)/shard_map/pallas_call | solution.py:185
  3.2 0.1 collective-permute-done.2.refs_4_
  3.3 0.0 collective-permute-done.1.refs_1_
  3.3 0.0 collective-permute-done.refs_3_.refs_1_
  3.3 1.1 %shard_map.59 = (f32[192,192]{1,0:T(8,128)S(1)}, f32[192,192]{1,0:T(8,128)S(1)}, f32[192,1]{1,0:T(8,128)S(1)}, f32[192,1]{1,0:T(8,128)S(1)}, f32[1,192]{1,0:T(1,...) custom-call(bf16[192,1024]{1,0:T(8,128)(2,1)S(1)} %get-tuple-element.17.refs_0_, ...), custom_call_target="tpu_custom_call" | custom-call | flops 301989888 | bytes 1 | tf_op jit(solution)/shard_map/pallas_call | solution.py:154
  4.4 2.6 %collective-permute-start.3 = (f32[1,128]{1,0:T(1,128)S(1)}, f32[1,128]{1,0:T(1,128)S(1)}, u32[]{:S(2)}, u32[]{:S(2)}) collective-permute-start(f32[1,128]{1,0:T(1,128)S(1)} %get-tuple-element.26), channel_id=1, source_target_pairs={{0,3},{1,2},{2,1},{3,0},{4,7},{5,6},{6,5},{7,4},{8,11},{9,10},{10,... | collective-permute-start | bytes 1544 | tf_op jit(solution)/shard_map/ppermute | solution.py:233
  7.0 1.3 %collective-permute-done.3 = f32[1,128]{1,0:T(1,128)S(1)} collective-permute-done((f32[1,128]{1,0:T(1,128)S(1)}, f32[1,128]{1,0:T(1,128)S(1)}, u32[]{:S(2)}, u32[]{:S(2)}) %collective-permute-start.3) | collective-permute-done | bytes 544 | tf_op jit(solution)/shard_map/ppermute | solution.py:233
  8.3 1.7 %collective-permute-start.4 = (f32[1,128]{1,0:T(1,128)S(1)}, f32[1,128]{1,0:T(1,128)S(1)}, u32[]{:S(2)}, u32[]{:S(2)}) collective-permute-start(f32[1,128]{1,0:T(1,128)S(1)} %add.12), channel_id=1, source_target_pairs={{0,5},{1,4},{2,7},{3,6},{4,1},{5,0},{6,3},{7,2},{8,13},{9,12},{10,... | collective-permute-start | bytes 1544 | tf_op jit(solution)/shard_map/ppermute | solution.py:233
  10.0 1.3 %collective-permute-done.4 = f32[1,128]{1,0:T(1,128)S(1)} collective-permute-done((f32[1,128]{1,0:T(1,128)S(1)}, f32[1,128]{1,0:T(1,128)S(1)}, u32[]{:S(2)}, u32[]{:S(2)}) %collective-permute-start.4) | collective-permute-done | bytes 544 | tf_op jit(solution)/shard_map/ppermute | solution.py:233
  11.3 1.8 %collective-permute-start.5 = (f32[1,128]{1,0:T(1,128)S(1)}, f32[1,128]{1,0:T(1,128)S(1)}, u32[]{:S(2)}, u32[]{:S(2)}) collective-permute-start(f32[1,128]{1,0:T(1,128)S(1)} %add.13), channel_id=1, source_target_pairs={{0,9},{1,8},{2,11},{3,10},{4,13},{5,12},{6,15},{7,14},{8,1},{9,0},... | collective-permute-start | bytes 1544 | tf_op jit(solution)/shard_map/ppermute | solution.py:233
  13.1 1.3 %shard_map.60 = f32[192,1024]{1,0:T(8,128)} custom-call(bf16[192,1024]{1,0:T(8,128)(2,1)S(1)} %get-tuple-element.15.refs_2_.refs_0_, bf16[192,1024]{1,0:T(8,128)(2,1)S(1)} %collective-permute-done.refs_3_.refs_1_, f32[192,192]{1,0:T(8,128)S(1)} %get-tuple-element.16.refs_5_.refs_2_, f32[192,192]{1,0:T(8,128)S(1)} %get-tuple-element.19.refs_3_, ...), custom_call_target="tpu_custom_call" | custom-call | flops 603979776 | bytes 1 | tf_op jit(solution)/shard_map/pallas_call | solution.py:154
  14.4 0.0 collective-permute-done.5
  14.4 2.7 %collective-permute-start.6 = (f32[1,128]{1,0:T(1,128)S(1)}, f32[1,128]{1,0:T(1,128)S(1)}, u32[]{:S(2)}, u32[]{:S(2)}) collective-permute-start(f32[1,128]{1,0:T(1,128)S(1)} %add.14), channel_id=1, source_target_pairs={{0,17},{1,16},{2,19},{3,18},{4,21},{5,20},{6,23},{7,22},{8,25},{9,... | collective-permute-start | bytes 1544 | tf_op jit(solution)/shard_map/ppermute | solution.py:233
  17.1 1.5 %shard_map.61 = f32[192,1024]{1,0:T(8,128)} custom-call(bf16[192,1024]{1,0:T(8,128)(2,1)S(1)} %get-tuple-element.17.refs_0_, bf16[192,1024]{1,0:T(8,128)(2,1)S(1)} %collective-permute-done.1.refs_1_, f32[192,192]{1,0:T(8,128)S(1)} %get-tuple-element.16.refs_5_.refs_2_, f32[192,192]{1,0:T(8,128)S(1)} %get-tuple-element.23.refs_3_, ...), custom_call_target="tpu_custom_call" | custom-call | flops 603979776 | bytes 1 | tf_op jit(solution)/shard_map/pallas_call | solution.py:154
  18.5 0.0 collective-permute-done.6
  18.5 0.5 %add.15 = f32[1,128]{1,0:T(1,128)} add(f32[1,128]{1,0:T(1,128)S(1)} %add.14, f32[1,128]{1,0:T(1,128)S(1)} %collective-permute-done.6) | non-fusion elementwise | flops 128 | bytes 1536 | tf_op jit(solution)/shard_map/add | solution.py:233
  (3 shorter events, 0.0 us)
Async XLA Ops:
  0.6 0.7 %copy-start = (s32[1,192]{1,0:T(1,128)S(1)}, s32[1,192]{1,0:T(1,128)}, u32[]{:S(2)}) copy-start(s32[1,192]{1,0:T(1,128)} %pair_ref.1) | copy-start | bytes 2308
  0.6 2.7 %collective-permute-start.1 = (bf16[192,1024]{1,0:T(8,128)(2,1)}, bf16[192,1024]{1,0:T(8,128)(2,1)S(1)}, u32[]{:S(2)}, u32[]{:S(2)}) collective-permute-start(bf16[192,1024]{1,0:T(8,128)(2,1)} %bitcast.7), channel_id=1, source_target_pairs={{0,1},{1,0},{2,3},{3,2},{4,5},{5,4},{6,7},{7,6},{8,9},{9,8},{10,11... | collective-permute-start | bytes 1179656 | tf_op jit(solution)/shard_map/ppermute | solution.py:174
  1.2 2.1 %collective-permute-start = (bf16[192,1024]{1,0:T(8,128)(2,1)}, bf16[192,1024]{1,0:T(8,128)(2,1)S(1)}, u32[]{:S(2)}, u32[]{:S(2)}) collective-permute-start(bf16[192,1024]{1,0:T(8,128)(2,1)} %bitcast.9), channel_id=1, source_target_pairs={{0,1},{1,0},{2,3},{3,2},{4,5},{5,4},{6,7},{7,6},{8,9},{9,8},{10,11... | collective-permute-start | bytes 1179656 | tf_op jit(solution)/shard_map/ppermute | solution.py:174
  1.3 2.0 %collective-permute-start.2 = (s32[1,192]{1,0:T(1,128)S(1)}, s32[1,192]{1,0:T(1,128)S(1)}, u32[]{:S(2)}, u32[]{:S(2)}) collective-permute-start(s32[1,192]{1,0:T(1,128)S(1)} %copy-done), channel_id=1, source_target_pairs={{0,1},{1,0},{2,3},{3,2},{4,5},{5,4},{6,7},{7,6},{8,9},{9,8},{10,11... | collective-permute-start | bytes 2312 | tf_op jit(solution)/shard_map/ppermute | solution.py:174
  4.4 3.9 %collective-permute-start.3 = (f32[1,128]{1,0:T(1,128)S(1)}, f32[1,128]{1,0:T(1,128)S(1)}, u32[]{:S(2)}, u32[]{:S(2)}) collective-permute-start(f32[1,128]{1,0:T(1,128)S(1)} %get-tuple-element.26), channel_id=1, source_target_pairs={{0,3},{1,2},{2,1},{3,0},{4,7},{5,6},{6,5},{7,4},{8,11},{9,10},{10,... | collective-permute-start | bytes 1544 | tf_op jit(solution)/shard_map/ppermute | solution.py:233
  8.3 3.0 %collective-permute-start.4 = (f32[1,128]{1,0:T(1,128)S(1)}, f32[1,128]{1,0:T(1,128)S(1)}, u32[]{:S(2)}, u32[]{:S(2)}) collective-permute-start(f32[1,128]{1,0:T(1,128)S(1)} %add.12), channel_id=1, source_target_pairs={{0,5},{1,4},{2,7},{3,6},{4,1},{5,0},{6,3},{7,2},{8,13},{9,12},{10,... | collective-permute-start | bytes 1544 | tf_op jit(solution)/shard_map/ppermute | solution.py:233
  11.3 3.1 %collective-permute-start.5 = (f32[1,128]{1,0:T(1,128)S(1)}, f32[1,128]{1,0:T(1,128)S(1)}, u32[]{:S(2)}, u32[]{:S(2)}) collective-permute-start(f32[1,128]{1,0:T(1,128)S(1)} %add.13), channel_id=1, source_target_pairs={{0,9},{1,8},{2,11},{3,10},{4,13},{5,12},{6,15},{7,14},{8,1},{9,0},... | collective-permute-start | bytes 1544 | tf_op jit(solution)/shard_map/ppermute | solution.py:233
  14.4 4.1 %collective-permute-start.6 = (f32[1,128]{1,0:T(1,128)S(1)}, f32[1,128]{1,0:T(1,128)S(1)}, u32[]{:S(2)}, u32[]{:S(2)}) collective-permute-start(f32[1,128]{1,0:T(1,128)S(1)} %add.14), channel_id=1, source_target_pairs={{0,17},{1,16},{2,19},{3,18},{4,21},{5,20},{6,23},{7,22},{8,25},{9,... | collective-permute-start | bytes 1544 | tf_op jit(solution)/shard_map/ppermute | solution.py:233

commit v3 on v2

v3 whole, which is shorter than its diff:
```python
import functools

import jax
import jax.numpy as jnp
from jax import lax
from jax.experimental import pallas as pl
from jax.experimental.pallas import tpu as pltpu
from jax.sharding import PartitionSpec as P


score_scale = 0.125
log2_e = 1.4426950408889634
grad_scale = score_scale * 0.5
kernel_vmem = 24 << 20
grad_blocks = 4
BOTH = ("blk", "grp")


def column_of(row):
    n = row.shape[1]
    eye = lax.broadcasted_iota(jnp.int32, (n, n), 0) == lax.broadcasted_iota(jnp.int32, (n, n), 1)
    spread = jnp.where(eye, jnp.broadcast_to(row.astype(jnp.float32), (n, n)), 0.0)
    return jnp.sum(spread, axis=1, keepdims=True).astype(jnp.int32)


def square(text, image):
    both_last = (((1,), (1,)), ((), ()))
    return lax.dot_general(text, image, both_last, preferred_element_type=jnp.float32) * (
        score_scale * log2_e
    )


def hit_of(count, pair_column, piece):
    rows = pair_column.shape[0]
    base = lax.rem(lax.axis_index("grp") + piece, count) * rows
    return pair_column - base == lax.broadcasted_iota(jnp.int32, (rows, rows), 1)


def own_kernel(count, *refs):
    text_hbm, image_hbm, pair_hbm, text_ref, image_ref, pair_column_ref, hit_ref, score_ref = refs[:8]
    pair_ref, sems = refs[8:]
    loads = [
        pltpu.make_async_copy(text_hbm, text_ref, sems.at[0]),
        pltpu.make_async_copy(image_hbm, image_ref, sems.at[1]),
        pltpu.make_async_copy(pair_hbm, pair_ref, sems.at[2]),
    ]
    for load in loads:
        load.start()
    loads[2].wait()
    pair_column_ref[...] = column_of(pair_ref[...])
    for load in loads[:2]:
        load.wait()
    score_ref[...] = square(text_ref[...], image_ref[...])
    hit_ref[...] = jnp.sum(hits_of(count, pair_column_ref, 0, score_ref), axis=1, keepdims=True)


def added(values):
    return functools.reduce(jnp.add, values)


def lse(line, axis):
    top = functools.reduce(jnp.maximum, [s[...] for s in line])
    top = jnp.max(top, axis=axis, keepdims=True)
    total = jnp.sum(added([jnp.exp2(s[...] - top) for s in line]), axis=axis, keepdims=True)
    return top + jnp.log(total) * log2_e


def hits_of(count, pair_column, piece, score):
    return jnp.where(hit_of(count, pair_column[...], piece), score[...], 0.0)


def stats_kernel(count, mean, *refs):
    refs = list(refs)

    def take(n):
        taken = refs[:n]
        del refs[:n]
        return taken

    texts, images, pairs = take(count), take(count), take(count - 1)
    own_pair, own_hit, own_score = take(3)
    col_scores, row_scores = take(count - 1), take(count - 1)
    row_lses, col_lses, pair_columns = take(count), take(count), take(count - 1)
    (part_ref,) = take(1)
    rest = take((count - 1) ** 2)

    members = range(count)
    rows = own_score.shape[0]
    columns = [own_pair, *pair_columns]
    for k in range(1, count):
        pair_columns[k - 1][...] = column_of(pairs[k - 1][...])
    scores = {(0, 0): own_score}
    for k in range(1, count):
        scores[k, 0] = col_scores[k - 1]
        scores[0, k] = row_scores[k - 1]
        for a in range(1, count):
            scores[a, k] = rest[(a - 1) * (count - 1) + k - 1]
    for b in members:
        line = [a for a in members if a or b]
        product = square(jnp.concatenate([texts[a][...] for a in line], axis=0), images[b][...])
        for n, a in enumerate(line):
            scores[a, b][...] = product[n * rows : (n + 1) * rows]

    for k in members:
        col_lses[k][...] = lse([scores[a, k] for a in members], 0)
        row_lses[k][...] = lse([scores[k, b] for b in members], 1)
    hits = []
    for a in members:
        pieces = [hits_of(count, columns[a], b, scores[a, b]) for b in members if a or b]
        hits.append(jnp.sum(added(pieces), axis=1, keepdims=True))
    hits[0] += own_hit[...]
    line = added([r[...] - 2.0 * h for r, h in zip(row_lses, hits)])
    cols = added([c[...] for c in col_lses])
    part = jnp.sum(line, axis=0, keepdims=True) + jnp.sum(cols, axis=1, keepdims=True)
    part_ref[...] = jnp.broadcast_to(part * mean, part_ref.shape)


def weight_of(score, row_lse, col_lse, hit):
    both = jnp.exp2(score - row_lse) + jnp.exp2(score - col_lse)
    return (both - jnp.where(hit, 2.0, 0.0)).astype(jnp.bfloat16)


def write_out(weights, pieces, dims, out_hbm, block_ref, sems):
    step = block_ref.shape[1] // sems.shape[0]
    stores = []
    for n in range(sems.shape[0]):
        at = slice(n * step, (n + 1) * step)
        terms = [
            lax.dot_general(w, p[:, at], (dims, ((), ())), preferred_element_type=jnp.float32)
            for w, p in zip(weights, pieces)
        ]
        block_ref[:, at] = added(terms) * grad_scale
        store = pltpu.make_async_copy(block_ref.at[:, at], out_hbm.at[:, at], sems.at[n])
        store.start()
        stores.append(store)
    for store in stores:
        store.wait()


def text_kernel(count, *refs):
    images, scores, cols = refs[:count], refs[count : 2 * count], refs[2 * count : 3 * count]
    row, pair, out_hbm, block_ref, sems = refs[3 * count :]
    weights = [
        weight_of(scores[k][...], row[...], cols[k][...], hit_of(count, pair[...], k))
        for k in range(count)
    ]
    write_out(weights, images, ((1,), (0,)), out_hbm, block_ref, sems)


def image_kernel(count, *refs):
    texts, scores, rows = refs[:count], refs[count : 2 * count], refs[2 * count : 3 * count]
    pairs = refs[3 * count : 4 * count]
    col, out_hbm, block_ref, sems = refs[4 * count :]
    weights = [
        weight_of(scores[k][...], rows[k][...], col[...], hit_of(count, pairs[k][...], 0))
        for k in range(count)
    ]
    write_out(weights, texts, ((0,), (0,)), out_hbm, block_ref, sems)


def in_vmem(n):
    return [pl.BlockSpec(memory_space=pltpu.VMEM)] * n


def call(kernel, out_shape, args, flops, scratch=(), out_space=pltpu.VMEM):
    single = not isinstance(out_shape, tuple)
    place = pl.BlockSpec(memory_space=out_space)
    return pl.pallas_call(
        kernel,
        out_shape=out_shape,
        in_specs=in_vmem(len(args)),
        out_specs=place if single else (place,) * len(out_shape),
        scratch_shapes=scratch,
        compiler_params=pltpu.CompilerParams(vmem_limit_bytes=kernel_vmem),
        cost_estimate=pl.CostEstimate(flops=flops, bytes_accessed=1, transcendentals=0),
    )(*[pltpu.with_memory_space_constraint(arg, pltpu.VMEM) for arg in args])


def rounds(blocks):
    bits = [1 << k for k in range(blocks.bit_length() - 1)]
    if len(bits) < 3:
        return [(bit,) for bit in bits]
    *near, third, second, first = bits
    return [(first | second,), (second | third, third, second), *[(bit,) for bit in near]]


def local(text, image, pair_index):
    count = lax.axis_size("grp")
    blocks = lax.axis_size("blk")
    rows, width = text.shape[1:]
    total = rows * count
    dot_flops = 2 * rows * rows * width

    def others(value):
        return [
            lax.ppermute(value, "grp", [(i, (i - k) % count) for i in range(count)])
            for k in range(1, count)
        ]

    def piece(shape, dtype=jnp.float32):
        return pltpu.VMEM(shape, dtype)

    other_pairs = others(pair_index)
    other_texts = others(text[0])
    other_images = others(image[0])

    own_text, own_image, own_pair, own_hit, own_score = pl.pallas_call(
        functools.partial(own_kernel, count),
        out_shape=(
            piece((rows, width), text.dtype),
            piece((rows, width), image.dtype),
            piece((rows, 1), jnp.int32),
            piece((rows, 1)),
            piece((rows, rows)),
        ),
        in_specs=[pl.BlockSpec(memory_space=pltpu.HBM)] * 3,
        out_specs=tuple(in_vmem(5)),
        scratch_shapes=[piece((1, rows), jnp.int32), pltpu.SemaphoreType.DMA((3,))],
        compiler_params=pltpu.CompilerParams(vmem_limit_bytes=kernel_vmem),
        cost_estimate=pl.CostEstimate(flops=4 * dot_flops, bytes_accessed=1, transcendentals=0),
    )(
        pltpu.with_memory_space_constraint(text[0], pltpu.HBM),
        pltpu.with_memory_space_constraint(image[0], pltpu.HBM),
        pltpu.with_memory_space_constraint(pair_index, pltpu.HBM),
    )

    texts = [own_text, *other_texts]
    images = [own_image, *other_images]
    line = [piece((rows, rows))] * (count - 1)
    results = call(
        functools.partial(stats_kernel, count, 1.0 / (2.0 * log2_e * total * blocks)),
        (
            *line,
            *line,
            *[piece((rows, 1))] * count,
            *[piece((1, rows))] * count,
            *[piece((rows, 1), jnp.int32)] * (count - 1),
            piece((1, 128)),
        ),
        [*texts, *images, *other_pairs, own_pair, own_hit, own_score],
        dot_flops * count * count,
        [piece((rows, rows))] * (count - 1) ** 2,
    )
    results = list(results)
    col_scores = [own_score, *results[: count - 1]]
    row_scores = [own_score, *results[count - 1 : 2 * count - 2]]
    results = results[2 * count - 2 :]
    row_lses, col_lses = results[:count], results[count : 2 * count]
    pairs = [own_pair, *results[2 * count : -1]]
    part = results[-1]

    if count == 2 and blocks & (blocks - 1) == 0:
        for flips in rounds(blocks):
            got = []
            for flip in flips:
                moves = [(i, i ^ (2 * flip + 1)) for i in range(blocks * count)]
                got.append(lax.ppermute(part, BOTH, moves))
            part = part + got[0] if len(got) == 1 else (part + got[1]) + (got[0] + got[2])
        loss = part[0, 0]
    else:
        loss = lax.psum(part[0, 0], BOTH) / count

    like = jax.ShapeDtypeStruct((rows, width), jnp.float32)
    stage = [piece((rows, width)), pltpu.SemaphoreType.DMA((grad_blocks,))]
    grad_text = call(
        functools.partial(text_kernel, count),
        like,
        [*images, *row_scores, *col_lses, row_lses[0], own_pair],
        4 * dot_flops * count,
        stage,
        pltpu.HBM,
    )
    grad_image = call(
        functools.partial(image_kernel, count),
        like,
        [*texts, *col_scores, *row_lses, *pairs, col_lses[0]],
        4 * dot_flops * count,
        stage,
        pltpu.HBM,
    )
    return grad_text[None], grad_image[None], loss


def solution(mesh):
    placed = (P("blk", "grp", None), P("blk", "grp", None), P("blk", "grp"))
    return jax.shard_map(
        local,
        mesh=mesh,
        in_specs=placed,
        out_specs=(P("blk", "grp", None), P("blk", "grp", None), P()),
        check_vma=False,
    )
```

time: 19.2 us -> 19.9 us (1.036)
  starting transfers between devices: 9.87 us -> 10.2 us
  waiting for transfers between devices: 2.7 us -> 3.03 us
    ppermute x4 -> x5, waiting for transfers between devices: 2.6 us -> 3.03 us  [local(): got.append(lax.ppermute(part, BOTH, moves))]
    ppermute x4 -> x5, starting transfers between devices: 8.74 us -> 9.08 us  [local(): got.append(lax.ppermute(part, BOTH, moves))]
    add x4 -> x3, other arithmetic: 0.52 us -> 0.52 us  [local(): part = part + got[0] if len(got) == 1 else part + got[1] + (got[0] + got[2])]
  transfers between devices with their start and end apart: 7 -> 8, of which waited for: 3 -> 3; matrix products, arithmetic and copies ran while one was open for 0% -> 0% of each run, Pallas kernels for 22% -> 21%
where the time goes in v3:
time: 19.9 us; the launch traced here: 19.7 us
  starting transfers between devices  10.2 us (51%)
  Pallas kernels  5.19 us (26%)
  waiting for transfers between devices  3.03 us (15%)
  between operations  0.71 us (4%)
  other arithmetic  0.52 us (3%)
    ppermute x5, starting transfers between devices, local(): got.append(lax.ppermute(part, BOTH, moves))  9.08 us
    pallas_call x3, Pallas kernels, call(): pl.pallas_call(kernel, out_shape=out_shape, in_specs=in_vmem(len(args)),...  3.67 us
    ppermute x5, waiting for transfers between devices, local(): got.append(lax.ppermute(part, BOTH, moves))  3.03 us
    pallas_call x1, Pallas kernels, local(): pl.pallas_call(functools.partial(own_kernel, count), out_shape=(piece((ro...  1.52 us
    ppermute x3, starting transfers between devices, others(): lax.ppermute(value, 'grp', [(i, (i - k) % count) for i in range(count)])  1.13 us
    add x3, other arithmetic, local(): part = part + got[0] if len(got) == 1 else part + got[1] + (got[0] + got[2])  0.52 us
  transfers between devices with their start and end apart: 8, of which 3 were waited for; matrix products, arithmetic and copies ran while one was open for 0% of the time, Pallas kernels for 21%

profile of v3, /device:TPU:0, one launch (start us, length us, event | category | flops | bytes accessed | tf_op | source)
XLA Modules:
  0.0 19.7 jit_solution(1195100753554065355)
XLA Ops:
  0.6 0.0 copy-start
  0.6 0.6 %collective-permute-start.1 = (bf16[192,1024]{1,0:T(8,128)(2,1)}, bf16[192,1024]{1,0:T(8,128)(2,1)S(1)}, u32[]{:S(2)}, u32[]{:S(2)}) collective-permute-start(bf16[192,1024]{1,0:T(8,128)(2,1)} %bitcast.7), channel_id=1, source_target_pairs={{0,1},{1,0},{2,3},{3,2},{4,5},{5,4},{6,7},{7,6},{8,9},{9,8},{10,11... | collective-permute-start | bytes 1179656 | tf_op jit(solution)/shard_map/ppermute | solution.py:196
  1.2 0.1 collective-permute-start
  1.3 0.0 copy-done
  1.3 0.5 %collective-permute-start.2 = (s32[1,192]{1,0:T(1,128)S(1)}, s32[1,192]{1,0:T(1,128)S(1)}, u32[]{:S(2)}, u32[]{:S(2)}) collective-permute-start(s32[1,192]{1,0:T(1,128)S(1)} %copy-done), channel_id=1, source_target_pairs={{0,1},{1,0},{2,3},{3,2},{4,5},{5,4},{6,7},{7,6},{8,9},{9,8},{10,11... | collective-permute-start | bytes 2312 | tf_op jit(solution)/shard_map/ppermute | solution.py:196
  1.8 1.5 %shard_map.58 = (bf16[192,1024]{1,0:T(8,128)(2,1)S(1)}, bf16[192,1024]{1,0:T(8,128)(2,1)S(1)}, s32[192,1]{1,0:T(8,128)S(1)}, f32[192,1]{1,0:T(8,128)S(1)}, f32[192,192]{1,0:T(8,128)S(1)}) custom-call(bf16[192,1024]{1,0:T(8,128)(2,1)} %bitcast.8, bf16[192,1024]{1,0:T(8,128)(2,1)} %bitcast.10, s32[1,192]{1,0:T(1,128)} %refs_2_.1), custom_call_target="tpu_custom_call" | custom-call | flops 301989888 | bytes 1 | tf_op jit(solution)/shard_map/pallas_call | solution.py:207
  3.3 0.0 collective-permute-done.2.refs_4_
  3.3 0.0 collective-permute-done.1.refs_1_
  3.4 0.0 collective-permute-done.refs_3_.refs_1_
  3.4 1.0 %shard_map.59 = (f32[192,192]{1,0:T(8,128)S(1)}, f32[192,192]{1,0:T(8,128)S(1)}, f32[192,1]{1,0:T(8,128)S(1)}, f32[192,1]{1,0:T(8,128)S(1)}, f32[1,192]{1,0:T(1,...) custom-call(bf16[192,1024]{1,0:T(8,128)(2,1)S(1)} %get-tuple-element.18.refs_0_, ...), custom_call_target="tpu_custom_call" | custom-call | flops 301989888 | bytes 1 | tf_op jit(solution)/shard_map/pallas_call | solution.py:168
  4.4 4.7 %collective-permute-start.3 = (f32[1,128]{1,0:T(1,128)S(1)}, f32[1,128]{1,0:T(1,128)S(1)}, u32[]{:S(2)}, u32[]{:S(2)}) collective-permute-start(f32[1,128]{1,0:T(1,128)S(1)} %get-tuple-element.28), channel_id=1, source_target_pairs={{0,25},{1,24},{2,27},{3,26},{4,29},{5,28},{6,31},{7,30},{8,17},{9,... | collective-permute-start | bytes 1544 | tf_op jit(solution)/shard_map/ppermute | solution.py:257
  9.1 1.3 %collective-permute-done.3 = f32[1,128]{1,0:T(1,128)S(1)} collective-permute-done((f32[1,128]{1,0:T(1,128)S(1)}, f32[1,128]{1,0:T(1,128)S(1)}, u32[]{:S(2)}, u32[]{:S(2)}) %collective-permute-start.3) | collective-permute-done | bytes 544 | tf_op jit(solution)/shard_map/ppermute | solution.py:257
  10.4 0.0 collective-permute-start.6
  10.4 2.8 %collective-permute-start.5 = (f32[1,128]{1,0:T(1,128)S(1)}, f32[1,128]{1,0:T(1,128)S(1)}, u32[]{:S(2)}, u32[]{:S(2)}) collective-permute-start(f32[1,128]{1,0:T(1,128)S(1)} %add.15), channel_id=1, source_target_pairs={{0,13},{1,12},{2,15},{3,14},{4,9},{5,8},{6,11},{7,10},{8,5},{9,4},... | collective-permute-start | bytes 1544 | tf_op jit(solution)/shard_map/ppermute | solution.py:257
  13.2 0.3 %collective-permute-start.4 = (f32[1,128]{1,0:T(1,128)S(1)}, f32[1,128]{1,0:T(1,128)S(1)}, u32[]{:S(2)}, u32[]{:S(2)}) collective-permute-start(f32[1,128]{1,0:T(1,128)S(1)} %add.15), channel_id=1, source_target_pairs={{0,5},{1,4},{2,7},{3,6},{4,1},{5,0},{6,3},{7,2},{8,13},{9,12},{10,... | collective-permute-start | bytes 1544 | tf_op jit(solution)/shard_map/ppermute | solution.py:257
  13.5 1.3 %shard_map.60 = f32[192,1024]{1,0:T(8,128)} custom-call(bf16[192,1024]{1,0:T(8,128)(2,1)S(1)} %get-tuple-element.16.refs_2_.refs_0_, bf16[192,1024]{1,0:T(8,128)(2,1)S(1)} %collective-permute-done.refs_3_.refs_1_, f32[192,192]{1,0:T(8,128)S(1)} %get-tuple-element.17.refs_7_.refs_2_, f32[192,192]{1,0:T(8,128)S(1)} %get-tuple-element.21.refs_3_, ...), custom_call_target="tpu_custom_call" | custom-call | flops 603979776 | bytes 1 | tf_op jit(solution)/shard_map/pallas_call | solution.py:168
  14.7 0.0 collective-permute-done.6
  14.7 0.0 collective-permute-done.5
  14.8 1.4 %collective-permute-done.4 = f32[1,128]{1,0:T(1,128)S(1)} collective-permute-done((f32[1,128]{1,0:T(1,128)S(1)}, f32[1,128]{1,0:T(1,128)S(1)}, u32[]{:S(2)}, u32[]{:S(2)}) %collective-permute-start.4) | collective-permute-done | bytes 544 | tf_op jit(solution)/shard_map/ppermute | solution.py:257
  16.2 1.3 %collective-permute-start.7 = (f32[1,128]{1,0:T(1,128)S(1)}, f32[1,128]{1,0:T(1,128)S(1)}, u32[]{:S(2)}, u32[]{:S(2)}) collective-permute-start(f32[1,128]{1,0:T(1,128)S(1)} %add_add_fusion), channel_id=1, source_target_pairs={{0,3},{1,2},{2,1},{3,0},{4,7},{5,6},{6,5},{7,4},{8,11},{9,10},{10,... | collective-permute-start | bytes 1544 | tf_op jit(solution)/shard_map/ppermute | solution.py:257
  17.5 1.4 %shard_map.61 = f32[192,1024]{1,0:T(8,128)} custom-call(bf16[192,1024]{1,0:T(8,128)(2,1)S(1)} %get-tuple-element.18.refs_0_, bf16[192,1024]{1,0:T(8,128)(2,1)S(1)} %collective-permute-done.1.refs_1_, f32[192,192]{1,0:T(8,128)S(1)} %get-tuple-element.17.refs_7_.refs_2_, f32[192,192]{1,0:T(8,128)S(1)} %get-tuple-element.25.refs_3_, ...), custom_call_target="tpu_custom_call" | custom-call | flops 603979776 | bytes 1 | tf_op jit(solution)/shard_map/pallas_call | solution.py:168
  18.9 0.3 %collective-permute-done.7 = f32[1,128]{1,0:T(1,128)S(1)} collective-permute-done((f32[1,128]{1,0:T(1,128)S(1)}, f32[1,128]{1,0:T(1,128)S(1)}, u32[]{:S(2)}, u32[]{:S(2)}) %collective-permute-start.7) | collective-permute-done | bytes 544 | tf_op jit(solution)/shard_map/ppermute | solution.py:257
  19.2 0.5 %add.19 = f32[1,128]{1,0:T(1,128)} add(f32[1,128]{1,0:T(1,128)S(1)} %add_add_fusion, f32[1,128]{1,0:T(1,128)S(1)} %collective-permute-done.7) | non-fusion elementwise | flops 128 | bytes 1536 | tf_op jit(solution)/shard_map/add | solution.py:258
  (2 shorter events, 0.0 us)
Async XLA Ops:
  0.6 0.7 %copy-start = (s32[1,192]{1,0:T(1,128)S(1)}, s32[1,192]{1,0:T(1,128)}, u32[]{:S(2)}) copy-start(s32[1,192]{1,0:T(1,128)} %refs_2_.1) | copy-start | bytes 2308
  0.6 2.7 %collective-permute-start.1 = (bf16[192,1024]{1,0:T(8,128)(2,1)}, bf16[192,1024]{1,0:T(8,128)(2,1)S(1)}, u32[]{:S(2)}, u32[]{:S(2)}) collective-permute-start(bf16[192,1024]{1,0:T(8,128)(2,1)} %bitcast.7), channel_id=1, source_target_pairs={{0,1},{1,0},{2,3},{3,2},{4,5},{5,4},{6,7},{7,6},{8,9},{9,8},{10,11... | collective-permute-start | bytes 1179656 | tf_op jit(solution)/shard_map/ppermute | solution.py:196
  1.2 2.2 %collective-permute-start = (bf16[192,1024]{1,0:T(8,128)(2,1)}, bf16[192,1024]{1,0:T(8,128)(2,1)S(1)}, u32[]{:S(2)}, u32[]{:S(2)}) collective-permute-start(bf16[192,1024]{1,0:T(8,128)(2,1)} %bitcast.9), channel_id=1, source_target_pairs={{0,1},{1,0},{2,3},{3,2},{4,5},{5,4},{6,7},{7,6},{8,9},{9,8},{10,11... | collective-permute-start | bytes 1179656 | tf_op jit(solution)/shard_map/ppermute | solution.py:196
  1.3 2.0 %collective-permute-start.2 = (s32[1,192]{1,0:T(1,128)S(1)}, s32[1,192]{1,0:T(1,128)S(1)}, u32[]{:S(2)}, u32[]{:S(2)}) collective-permute-start(s32[1,192]{1,0:T(1,128)S(1)} %copy-done), channel_id=1, source_target_pairs={{0,1},{1,0},{2,3},{3,2},{4,5},{5,4},{6,7},{7,6},{8,9},{9,8},{10,11... | collective-permute-start | bytes 2312 | tf_op jit(solution)/shard_map/ppermute | solution.py:196
  4.4 6.0 %collective-permute-start.3 = (f32[1,128]{1,0:T(1,128)S(1)}, f32[1,128]{1,0:T(1,128)S(1)}, u32[]{:S(2)}, u32[]{:S(2)}) collective-permute-start(f32[1,128]{1,0:T(1,128)S(1)} %get-tuple-element.28), channel_id=1, source_target_pairs={{0,25},{1,24},{2,27},{3,26},{4,29},{5,28},{6,31},{7,30},{8,17},{9,... | collective-permute-start | bytes 1544 | tf_op jit(solution)/shard_map/ppermute | solution.py:257
  10.4 4.4 %collective-permute-start.6 = (f32[1,128]{1,0:T(1,128)S(1)}, f32[1,128]{1,0:T(1,128)S(1)}, u32[]{:S(2)}, u32[]{:S(2)}) collective-permute-start(f32[1,128]{1,0:T(1,128)S(1)} %add.15), channel_id=1, source_target_pairs={{0,9},{1,8},{2,11},{3,10},{4,13},{5,12},{6,15},{7,14},{8,1},{9,0},... | collective-permute-start | bytes 1544 | tf_op jit(solution)/shard_map/ppermute | solution.py:257
  10.4 4.4 %collective-permute-start.5 = (f32[1,128]{1,0:T(1,128)S(1)}, f32[1,128]{1,0:T(1,128)S(1)}, u32[]{:S(2)}, u32[]{:S(2)}) collective-permute-start(f32[1,128]{1,0:T(1,128)S(1)} %add.15), channel_id=1, source_target_pairs={{0,13},{1,12},{2,15},{3,14},{4,9},{5,8},{6,11},{7,10},{8,5},{9,4},... | collective-permute-start | bytes 1544 | tf_op jit(solution)/shard_map/ppermute | solution.py:257
  13.2 3.0 %collective-permute-start.4 = (f32[1,128]{1,0:T(1,128)S(1)}, f32[1,128]{1,0:T(1,128)S(1)}, u32[]{:S(2)}, u32[]{:S(2)}) collective-permute-start(f32[1,128]{1,0:T(1,128)S(1)} %add.15), channel_id=1, source_target_pairs={{0,5},{1,4},{2,7},{3,6},{4,1},{5,0},{6,3},{7,2},{8,13},{9,12},{10,... | collective-permute-start | bytes 1544 | tf_op jit(solution)/shard_map/ppermute | solution.py:257
  16.2 3.0 %collective-permute-start.7 = (f32[1,128]{1,0:T(1,128)S(1)}, f32[1,128]{1,0:T(1,128)S(1)}, u32[]{:S(2)}, u32[]{:S(2)}) collective-permute-start(f32[1,128]{1,0:T(1,128)S(1)} %add_add_fusion), channel_id=1, source_target_pairs={{0,3},{1,2},{2,1},{3,0},{4,7},{5,6},{6,5},{7,4},{8,11},{9,10},{10,... | collective-permute-start | bytes 1544 | tf_op jit(solution)/shard_map/ppermute | solution.py:257

commit v4 on v3

--- a/solution.py
+++ b/solution.py
@@ -51,7 +51,7 @@
     for load in loads[:2]:
         load.wait()
     score_ref[...] = square(text_ref[...], image_ref[...])
-    hit_ref[...] = jnp.sum(hits_of(count, pair_column_ref, 0, score_ref), axis=1, keepdims=True)
+    hit_ref[...] = jnp.sum(hits_of(count, pair_column_ref, 0, score_ref), axis=0, keepdims=True)
 
 
 def added(values):
@@ -105,13 +105,13 @@
         col_lses[k][...] = lse([scores[a, k] for a in members], 0)
         row_lses[k][...] = lse([scores[k, b] for b in members], 1)
     hits = []
-    for a in members:
-        pieces = [hits_of(count, columns[a], b, scores[a, b]) for b in members if a or b]
-        hits.append(jnp.sum(added(pieces), axis=1, keepdims=True))
+    for b in members:
+        pieces = [hits_of(count, columns[a], b, scores[a, b]) for a in members if a or b]
+        hits.append(jnp.sum(added(pieces), axis=0, keepdims=True))
     hits[0] += own_hit[...]
-    line = added([r[...] - 2.0 * h for r, h in zip(row_lses, hits)])
-    cols = added([c[...] for c in col_lses])
-    part = jnp.sum(line, axis=0, keepdims=True) + jnp.sum(cols, axis=1, keepdims=True)
+    cols = added([c[...] - 2.0 * h for c, h in zip(col_lses, hits)])
+    line = jnp.sum(added([r[...] for r in row_lses]), axis=0, keepdims=True)
+    part = line + jnp.sum(cols, axis=1, keepdims=True)
     part_ref[...] = jnp.broadcast_to(part * mean, part_ref.shape)
 
 
@@ -210,7 +210,7 @@
             piece((rows, width), text.dtype),
             piece((rows, width), image.dtype),
             piece((rows, 1), jnp.int32),
-            piece((rows, 1)),
+            piece((1, rows)),
             piece((rows, rows)),
         ),
         in_specs=[pl.BlockSpec(memory_space=pltpu.HBM)] * 3,

time: 19.9 us -> 19.9 us (level)
  transfers between devices with their start and end apart: 8 -> 8, of which waited for: 3 -> 4; matrix products, arithmetic and copies ran while one was open for 0% -> 0% of each run, Pallas kernels for 21% -> 21%
where the time goes in v4:
time: 19.9 us; the launch traced here: 19.8 us
  starting transfers between devices  10.2 us (51%)
  Pallas kernels  5.21 us (26%)
  waiting for transfers between devices  3.06 us (15%)
  between operations  0.69 us (3%)
  other arithmetic  0.52 us (3%)
    ppermute x5, starting transfers between devices, local(): got.append(lax.ppermute(part, BOTH, moves))  9.12 us
    pallas_call x3, Pallas kernels, call(): pl.pallas_call(kernel, out_shape=out_shape, in_specs=in_vmem(len(args)),...  3.75 us
    ppermute x5, waiting for transfers between devices, local(): got.append(lax.ppermute(part, BOTH, moves))  3 us
    pallas_call x1, Pallas kernels, local(): pl.pallas_call(functools.partial(own_kernel, count), out_shape=(piece((ro...  1.46 us
    ppermute x3, starting transfers between devices, others(): lax.ppermute(value, 'grp', [(i, (i - k) % count) for i in range(count)])  1.13 us
    add x3, other arithmetic, local(): part = part + got[0] if len(got) == 1 else part + got[1] + (got[0] + got[2])  0.52 us
  transfers between devices with their start and end apart: 8, of which 4 were waited for; matrix products, arithmetic and copies ran while one was open for 0% of the time, Pallas kernels for 21%

profile of v4, /device:TPU:0, one launch (start us, length us, event | category | flops | bytes accessed | tf_op | source)
XLA Modules:
  0.0 19.8 jit_solution(13714163874600293952)
XLA Ops:
  0.6 0.0 copy-start
  0.6 0.6 %collective-permute-start.1 = (bf16[192,1024]{1,0:T(8,128)(2,1)}, bf16[192,1024]{1,0:T(8,128)(2,1)S(1)}, u32[]{:S(2)}, u32[]{:S(2)}) collective-permute-start(bf16[192,1024]{1,0:T(8,128)(2,1)} %bitcast.7), channel_id=1, source_target_pairs={{0,1},{1,0},{2,3},{3,2},{4,5},{5,4},{6,7},{7,6},{8,9},{9,8},{10,11... | collective-permute-start | bytes 1179656 | tf_op jit(solution)/shard_map/ppermute | solution.py:196
  1.2 0.1 collective-permute-start
  1.3 0.0 copy-done
  1.3 0.5 %collective-permute-start.2 = (s32[1,192]{1,0:T(1,128)S(1)}, s32[1,192]{1,0:T(1,128)S(1)}, u32[]{:S(2)}, u32[]{:S(2)}) collective-permute-start(s32[1,192]{1,0:T(1,128)S(1)} %copy-done), channel_id=1, source_target_pairs={{0,1},{1,0},{2,3},{3,2},{4,5},{5,4},{6,7},{7,6},{8,9},{9,8},{10,11... | collective-permute-start | bytes 2312 | tf_op jit(solution)/shard_map/ppermute | solution.py:196
  1.8 1.5 %shard_map.58 = (bf16[192,1024]{1,0:T(8,128)(2,1)S(1)}, bf16[192,1024]{1,0:T(8,128)(2,1)S(1)}, s32[192,1]{1,0:T(8,128)S(1)}, f32[1,192]{1,0:T(1,128)S(1)}, f32[192,192]{1,0:T(8,128)S(1)}) custom-call(bf16[192,1024]{1,0:T(8,128)(2,1)} %bitcast.8, bf16[192,1024]{1,0:T(8,128)(2,1)} %bitcast.10, s32[1,192]{1,0:T(1,128)} %refs_2_.1), custom_call_target="tpu_custom_call" | custom-call | flops 301989888 | bytes 1 | tf_op jit(solution)/shard_map/pallas_call | solution.py:207
  3.3 0.1 collective-permute-done.2.refs_4_
  3.3 0.0 collective-permute-done.1.refs_1_
  3.3 0.0 collective-permute-done.refs_3_.refs_1_
  3.3 1.1 %shard_map.59 = (f32[192,192]{1,0:T(8,128)S(1)}, f32[192,192]{1,0:T(8,128)S(1)}, f32[192,1]{1,0:T(8,128)S(1)}, f32[192,1]{1,0:T(8,128)S(1)}, f32[1,192]{1,0:T(1,...) custom-call(bf16[192,1024]{1,0:T(8,128)(2,1)S(1)} %get-tuple-element.18.refs_0_, ...), custom_call_target="tpu_custom_call" | custom-call | flops 301989888 | bytes 1 | tf_op jit(solution)/shard_map/pallas_call | solution.py:168
  4.4 4.7 %collective-permute-start.3 = (f32[1,128]{1,0:T(1,128)S(1)}, f32[1,128]{1,0:T(1,128)S(1)}, u32[]{:S(2)}, u32[]{:S(2)}) collective-permute-start(f32[1,128]{1,0:T(1,128)S(1)} %get-tuple-element.28), channel_id=1, source_target_pairs={{0,25},{1,24},{2,27},{3,26},{4,29},{5,28},{6,31},{7,30},{8,17},{9,... | collective-permute-start | bytes 1544 | tf_op jit(solution)/shard_map/ppermute | solution.py:257
  9.1 1.3 %collective-permute-done.3 = f32[1,128]{1,0:T(1,128)S(1)} collective-permute-done((f32[1,128]{1,0:T(1,128)S(1)}, f32[1,128]{1,0:T(1,128)S(1)}, u32[]{:S(2)}, u32[]{:S(2)}) %collective-permute-start.3) | collective-permute-done | bytes 544 | tf_op jit(solution)/shard_map/ppermute | solution.py:257
  10.4 0.0 collective-permute-start.6
  10.4 2.9 %collective-permute-start.5 = (f32[1,128]{1,0:T(1,128)S(1)}, f32[1,128]{1,0:T(1,128)S(1)}, u32[]{:S(2)}, u32[]{:S(2)}) collective-permute-start(f32[1,128]{1,0:T(1,128)S(1)} %add.15), channel_id=1, source_target_pairs={{0,13},{1,12},{2,15},{3,14},{4,9},{5,8},{6,11},{7,10},{8,5},{9,4},... | collective-permute-start | bytes 1544 | tf_op jit(solution)/shard_map/ppermute | solution.py:257
  13.2 0.3 %collective-permute-start.4 = (f32[1,128]{1,0:T(1,128)S(1)}, f32[1,128]{1,0:T(1,128)S(1)}, u32[]{:S(2)}, u32[]{:S(2)}) collective-permute-start(f32[1,128]{1,0:T(1,128)S(1)} %add.15), channel_id=1, source_target_pairs={{0,5},{1,4},{2,7},{3,6},{4,1},{5,0},{6,3},{7,2},{8,13},{9,12},{10,... | collective-permute-start | bytes 1544 | tf_op jit(solution)/shard_map/ppermute | solution.py:257
  13.5 1.3 %shard_map.60 = f32[192,1024]{1,0:T(8,128)} custom-call(bf16[192,1024]{1,0:T(8,128)(2,1)S(1)} %get-tuple-element.16.refs_2_.refs_0_, bf16[192,1024]{1,0:T(8,128)(2,1)S(1)} %collective-permute-done.refs_3_.refs_1_, f32[192,192]{1,0:T(8,128)S(1)} %get-tuple-element.17.refs_7_.refs_2_, f32[192,192]{1,0:T(8,128)S(1)} %get-tuple-element.21.refs_3_, ...), custom_call_target="tpu_custom_call" | custom-call | flops 603979776 | bytes 1 | tf_op jit(solution)/shard_map/pallas_call | solution.py:168
  14.8 0.0 collective-permute-done.6
  14.8 0.0 collective-permute-done.5
  14.8 1.4 %collective-permute-done.4 = f32[1,128]{1,0:T(1,128)S(1)} collective-permute-done((f32[1,128]{1,0:T(1,128)S(1)}, f32[1,128]{1,0:T(1,128)S(1)}, u32[]{:S(2)}, u32[]{:S(2)}) %collective-permute-start.4) | collective-permute-done | bytes 544 | tf_op jit(solution)/shard_map/ppermute | solution.py:257
  16.2 1.3 %collective-permute-start.7 = (f32[1,128]{1,0:T(1,128)S(1)}, f32[1,128]{1,0:T(1,128)S(1)}, u32[]{:S(2)}, u32[]{:S(2)}) collective-permute-start(f32[1,128]{1,0:T(1,128)S(1)} %add_add_fusion), channel_id=1, source_target_pairs={{0,3},{1,2},{2,1},{3,0},{4,7},{5,6},{6,5},{7,4},{8,11},{9,10},{10,... | collective-permute-start | bytes 1544 | tf_op jit(solution)/shard_map/ppermute | solution.py:257
  17.5 1.4 %shard_map.61 = f32[192,1024]{1,0:T(8,128)} custom-call(bf16[192,1024]{1,0:T(8,128)(2,1)S(1)} %get-tuple-element.18.refs_0_, bf16[192,1024]{1,0:T(8,128)(2,1)S(1)} %collective-permute-done.1.refs_1_, f32[192,192]{1,0:T(8,128)S(1)} %get-tuple-element.17.refs_7_.refs_2_, f32[192,192]{1,0:T(8,128)S(1)} %get-tuple-element.25.refs_3_, ...), custom_call_target="tpu_custom_call" | custom-call | flops 603979776 | bytes 1 | tf_op jit(solution)/shard_map/pallas_call | solution.py:168
  19.0 0.3 %collective-permute-done.7 = f32[1,128]{1,0:T(1,128)S(1)} collective-permute-done((f32[1,128]{1,0:T(1,128)S(1)}, f32[1,128]{1,0:T(1,128)S(1)}, u32[]{:S(2)}, u32[]{:S(2)}) %collective-permute-start.7) | collective-permute-done | bytes 544 | tf_op jit(solution)/shard_map/ppermute | solution.py:257
  19.2 0.5 %add.19 = f32[1,128]{1,0:T(1,128)} add(f32[1,128]{1,0:T(1,128)S(1)} %add_add_fusion, f32[1,128]{1,0:T(1,128)S(1)} %collective-permute-done.7) | non-fusion elementwise | flops 128 | bytes 1536 | tf_op jit(solution)/shard_map/add | solution.py:258
  (2 shorter events, 0.0 us)
Async XLA Ops:
  0.6 0.7 %copy-start = (s32[1,192]{1,0:T(1,128)S(1)}, s32[1,192]{1,0:T(1,128)}, u32[]{:S(2)}) copy-start(s32[1,192]{1,0:T(1,128)} %refs_2_.1) | copy-start | bytes 2308
  0.6 2.7 %collective-permute-start.1 = (bf16[192,1024]{1,0:T(8,128)(2,1)}, bf16[192,1024]{1,0:T(8,128)(2,1)S(1)}, u32[]{:S(2)}, u32[]{:S(2)}) collective-permute-start(bf16[192,1024]{1,0:T(8,128)(2,1)} %bitcast.7), channel_id=1, source_target_pairs={{0,1},{1,0},{2,3},{3,2},{4,5},{5,4},{6,7},{7,6},{8,9},{9,8},{10,11... | collective-permute-start | bytes 1179656 | tf_op jit(solution)/shard_map/ppermute | solution.py:196
  1.2 2.1 %collective-permute-start = (bf16[192,1024]{1,0:T(8,128)(2,1)}, bf16[192,1024]{1,0:T(8,128)(2,1)S(1)}, u32[]{:S(2)}, u32[]{:S(2)}) collective-permute-start(bf16[192,1024]{1,0:T(8,128)(2,1)} %bitcast.9), channel_id=1, source_target_pairs={{0,1},{1,0},{2,3},{3,2},{4,5},{5,4},{6,7},{7,6},{8,9},{9,8},{10,11... | collective-permute-start | bytes 1179656 | tf_op jit(solution)/shard_map/ppermute | solution.py:196
  1.3 2.0 %collective-permute-start.2 = (s32[1,192]{1,0:T(1,128)S(1)}, s32[1,192]{1,0:T(1,128)S(1)}, u32[]{:S(2)}, u32[]{:S(2)}) collective-permute-start(s32[1,192]{1,0:T(1,128)S(1)} %copy-done), channel_id=1, source_target_pairs={{0,1},{1,0},{2,3},{3,2},{4,5},{5,4},{6,7},{7,6},{8,9},{9,8},{10,11... | collective-permute-start | bytes 2312 | tf_op jit(solution)/shard_map/ppermute | solution.py:196
  4.4 6.0 %collective-permute-start.3 = (f32[1,128]{1,0:T(1,128)S(1)}, f32[1,128]{1,0:T(1,128)S(1)}, u32[]{:S(2)}, u32[]{:S(2)}) collective-permute-start(f32[1,128]{1,0:T(1,128)S(1)} %get-tuple-element.28), channel_id=1, source_target_pairs={{0,25},{1,24},{2,27},{3,26},{4,29},{5,28},{6,31},{7,30},{8,17},{9,... | collective-permute-start | bytes 1544 | tf_op jit(solution)/shard_map/ppermute | solution.py:257
  10.4 4.4 %collective-permute-start.6 = (f32[1,128]{1,0:T(1,128)S(1)}, f32[1,128]{1,0:T(1,128)S(1)}, u32[]{:S(2)}, u32[]{:S(2)}) collective-permute-start(f32[1,128]{1,0:T(1,128)S(1)} %add.15), channel_id=1, source_target_pairs={{0,9},{1,8},{2,11},{3,10},{4,13},{5,12},{6,15},{7,14},{8,1},{9,0},... | collective-permute-start | bytes 1544 | tf_op jit(solution)/shard_map/ppermute | solution.py:257
  10.4 4.4 %collective-permute-start.5 = (f32[1,128]{1,0:T(1,128)S(1)}, f32[1,128]{1,0:T(1,128)S(1)}, u32[]{:S(2)}, u32[]{:S(2)}) collective-permute-start(f32[1,128]{1,0:T(1,128)S(1)} %add.15), channel_id=1, source_target_pairs={{0,13},{1,12},{2,15},{3,14},{4,9},{5,8},{6,11},{7,10},{8,5},{9,4},... | collective-permute-start | bytes 1544 | tf_op jit(solution)/shard_map/ppermute | solution.py:257
  13.2 3.0 %collective-permute-start.4 = (f32[1,128]{1,0:T(1,128)S(1)}, f32[1,128]{1,0:T(1,128)S(1)}, u32[]{:S(2)}, u32[]{:S(2)}) collective-permute-start(f32[1,128]{1,0:T(1,128)S(1)} %add.15), channel_id=1, source_target_pairs={{0,5},{1,4},{2,7},{3,6},{4,1},{5,0},{6,3},{7,2},{8,13},{9,12},{10,... | collective-permute-start | bytes 1544 | tf_op jit(solution)/shard_map/ppermute | solution.py:257
  16.2 3.0 %collective-permute-start.7 = (f32[1,128]{1,0:T(1,128)S(1)}, f32[1,128]{1,0:T(1,128)S(1)}, u32[]{:S(2)}, u32[]{:S(2)}) collective-permute-start(f32[1,128]{1,0:T(1,128)S(1)} %add_add_fusion), channel_id=1, source_target_pairs={{0,3},{1,2},{2,1},{3,0},{4,7},{5,6},{6,5},{7,4},{8,11},{9,10},{10,... | collective-permute-start | bytes 1544 | tf_op jit(solution)/shard_map/ppermute | solution.py:257

commit v5 on v4

--- a/solution.py
+++ b/solution.py
@@ -20,7 +20,7 @@
     n = row.shape[1]
     eye = lax.broadcasted_iota(jnp.int32, (n, n), 0) == lax.broadcasted_iota(jnp.int32, (n, n), 1)
     spread = jnp.where(eye, jnp.broadcast_to(row.astype(jnp.float32), (n, n)), 0.0)
-    return jnp.sum(spread, axis=1, keepdims=True).astype(jnp.int32)
+    return jnp.sum(spread, axis=1, keepdims=True)
 
 
 def square(text, image):
@@ -33,7 +33,8 @@
 def hit_of(count, pair_column, piece):
     rows = pair_column.shape[0]
     base = lax.rem(lax.axis_index("grp") + piece, count) * rows
-    return pair_column - base == lax.broadcasted_iota(jnp.int32, (rows, rows), 1)
+    ids = lax.broadcasted_iota(jnp.int32, (1, rows), 1) + base
+    return pair_column == ids.astype(jnp.float32)
 
 
 def own_kernel(count, *refs):
@@ -209,7 +210,7 @@
         out_shape=(
             piece((rows, width), text.dtype),
             piece((rows, width), image.dtype),
-            piece((rows, 1), jnp.int32),
+            piece((rows, 1)),
             piece((1, rows)),
             piece((rows, rows)),
         ),
@@ -234,7 +235,7 @@
             *line,
             *[piece((rows, 1))] * count,
             *[piece((1, rows))] * count,
-            *[piece((rows, 1), jnp.int32)] * (count - 1),
+            *[piece((rows, 1))] * (count - 1),
             piece((1, 128)),
         ),
         [*texts, *images, *other_pairs, own_pair, own_hit, own_score],

time: 19.9 us -> 19.9 us (level)
  no operation moved by 1% of the time
where the time goes in v5:
time: 19.9 us; the launch traced here: 19.7 us
  starting transfers between devices  10.3 us (52%)
  Pallas kernels  5.2 us (26%)
  waiting for transfers between devices  3.03 us (15%)
  between operations  0.69 us (3%)
  other arithmetic  0.52 us (3%)
    ppermute x5, starting transfers between devices, local(): got.append(lax.ppermute(part, BOTH, moves))  9.13 us
    pallas_call x3, Pallas kernels, call(): pl.pallas_call(kernel, out_shape=out_shape, in_specs=in_vmem(len(args)),...  3.74 us
    ppermute x5, waiting for transfers between devices, local(): got.append(lax.ppermute(part, BOTH, moves))  2.97 us
    pallas_call x1, Pallas kernels, local(): pl.pallas_call(functools.partial(own_kernel, count), out_shape=(piece((ro...  1.45 us
    ppermute x3, starting transfers between devices, others(): lax.ppermute(value, 'grp', [(i, (i - k) % count) for i in range(count)])  1.13 us
    add x3, other arithmetic, local(): part = part + got[0] if len(got) == 1 else part + got[1] + (got[0] + got[2])  0.52 us
  transfers between devices with their start and end apart: 8, of which 4 were waited for; matrix products, arithmetic and copies ran while one was open for 0% of the time, Pallas kernels for 21%

profile of v5, /device:TPU:0, one launch (start us, length us, event | category | flops | bytes accessed | tf_op | source)
XLA Modules:
  0.0 19.7 jit_solution(17090214316634939719)
XLA Ops:
  0.6 0.0 copy-start
  0.6 0.6 %collective-permute-start.1 = (bf16[192,1024]{1,0:T(8,128)(2,1)}, bf16[192,1024]{1,0:T(8,128)(2,1)S(1)}, u32[]{:S(2)}, u32[]{:S(2)}) collective-permute-start(bf16[192,1024]{1,0:T(8,128)(2,1)} %bitcast.7), channel_id=1, source_target_pairs={{0,1},{1,0},{2,3},{3,2},{4,5},{5,4},{6,7},{7,6},{8,9},{9,8},{10,11... | collective-permute-start | bytes 1179656 | tf_op jit(solution)/shard_map/ppermute | solution.py:197
  1.2 0.1 collective-permute-start
  1.3 0.0 copy-done
  1.3 0.5 %collective-permute-start.2 = (s32[1,192]{1,0:T(1,128)S(1)}, s32[1,192]{1,0:T(1,128)S(1)}, u32[]{:S(2)}, u32[]{:S(2)}) collective-permute-start(s32[1,192]{1,0:T(1,128)S(1)} %copy-done), channel_id=1, source_target_pairs={{0,1},{1,0},{2,3},{3,2},{4,5},{5,4},{6,7},{7,6},{8,9},{9,8},{10,11... | collective-permute-start | bytes 2312 | tf_op jit(solution)/shard_map/ppermute | solution.py:197
  1.8 1.5 %shard_map.58 = (bf16[192,1024]{1,0:T(8,128)(2,1)S(1)}, bf16[192,1024]{1,0:T(8,128)(2,1)S(1)}, f32[192,1]{1,0:T(8,128)S(1)}, f32[1,192]{1,0:T(1,128)S(1)}, f32[192,192]{1,0:T(8,128)S(1)}) custom-call(bf16[192,1024]{1,0:T(8,128)(2,1)} %bitcast.8, bf16[192,1024]{1,0:T(8,128)(2,1)} %bitcast.10, s32[1,192]{1,0:T(1,128)} %refs_2_.1), custom_call_target="tpu_custom_call" | custom-call | flops 301989888 | bytes 1 | tf_op jit(solution)/shard_map/pallas_call | solution.py:208
  3.3 0.1 collective-permute-done.2.refs_4_
  3.3 0.0 collective-permute-done.1.refs_1_
  3.3 0.0 collective-permute-done.refs_3_.refs_1_
  3.3 1.0 %shard_map.59 = (f32[192,192]{1,0:T(8,128)S(1)}, f32[192,192]{1,0:T(8,128)S(1)}, f32[192,1]{1,0:T(8,128)S(1)}, f32[192,1]{1,0:T(8,128)S(1)}, f32[1,192]{1,0:T(1,...) custom-call(bf16[192,1024]{1,0:T(8,128)(2,1)S(1)} %get-tuple-element.18.refs_0_, ...), custom_call_target="tpu_custom_call" | custom-call | flops 301989888 | bytes 1 | tf_op jit(solution)/shard_map/pallas_call | solution.py:169
  4.4 4.7 %collective-permute-start.3 = (f32[1,128]{1,0:T(1,128)S(1)}, f32[1,128]{1,0:T(1,128)S(1)}, u32[]{:S(2)}, u32[]{:S(2)}) collective-permute-start(f32[1,128]{1,0:T(1,128)S(1)} %get-tuple-element.28), channel_id=1, source_target_pairs={{0,25},{1,24},{2,27},{3,26},{4,29},{5,28},{6,31},{7,30},{8,17},{9,... | collective-permute-start | bytes 1544 | tf_op jit(solution)/shard_map/ppermute | solution.py:258
  9.1 1.3 %collective-permute-done.3 = f32[1,128]{1,0:T(1,128)S(1)} collective-permute-done((f32[1,128]{1,0:T(1,128)S(1)}, f32[1,128]{1,0:T(1,128)S(1)}, u32[]{:S(2)}, u32[]{:S(2)}) %collective-permute-start.3) | collective-permute-done | bytes 544 | tf_op jit(solution)/shard_map/ppermute | solution.py:258
  10.4 0.0 collective-permute-start.6
  10.4 2.8 %collective-permute-start.5 = (f32[1,128]{1,0:T(1,128)S(1)}, f32[1,128]{1,0:T(1,128)S(1)}, u32[]{:S(2)}, u32[]{:S(2)}) collective-permute-start(f32[1,128]{1,0:T(1,128)S(1)} %add.15), channel_id=1, source_target_pairs={{0,13},{1,12},{2,15},{3,14},{4,9},{5,8},{6,11},{7,10},{8,5},{9,4},... | collective-permute-start | bytes 1544 | tf_op jit(solution)/shard_map/ppermute | solution.py:258
  13.2 0.3 %collective-permute-start.4 = (f32[1,128]{1,0:T(1,128)S(1)}, f32[1,128]{1,0:T(1,128)S(1)}, u32[]{:S(2)}, u32[]{:S(2)}) collective-permute-start(f32[1,128]{1,0:T(1,128)S(1)} %add.15), channel_id=1, source_target_pairs={{0,5},{1,4},{2,7},{3,6},{4,1},{5,0},{6,3},{7,2},{8,13},{9,12},{10,... | collective-permute-start | bytes 1544 | tf_op jit(solution)/shard_map/ppermute | solution.py:258
  13.5 1.3 %shard_map.60 = f32[192,1024]{1,0:T(8,128)} custom-call(bf16[192,1024]{1,0:T(8,128)(2,1)S(1)} %get-tuple-element.16.refs_2_.refs_0_, bf16[192,1024]{1,0:T(8,128)(2,1)S(1)} %collective-permute-done.refs_3_.refs_1_, f32[192,192]{1,0:T(8,128)S(1)} %get-tuple-element.17.refs_7_.refs_2_, f32[192,192]{1,0:T(8,128)S(1)} %get-tuple-element.21.refs_3_, ...), custom_call_target="tpu_custom_call" | custom-call | flops 603979776 | bytes 1 | tf_op jit(solution)/shard_map/pallas_call | solution.py:169
  14.8 0.0 collective-permute-done.6
  14.8 0.0 collective-permute-done.5
  14.8 1.4 %collective-permute-done.4 = f32[1,128]{1,0:T(1,128)S(1)} collective-permute-done((f32[1,128]{1,0:T(1,128)S(1)}, f32[1,128]{1,0:T(1,128)S(1)}, u32[]{:S(2)}, u32[]{:S(2)}) %collective-permute-start.4) | collective-permute-done | bytes 544 | tf_op jit(solution)/shard_map/ppermute | solution.py:258
  16.2 1.3 %collective-permute-start.7 = (f32[1,128]{1,0:T(1,128)S(1)}, f32[1,128]{1,0:T(1,128)S(1)}, u32[]{:S(2)}, u32[]{:S(2)}) collective-permute-start(f32[1,128]{1,0:T(1,128)S(1)} %add_add_fusion), channel_id=1, source_target_pairs={{0,3},{1,2},{2,1},{3,0},{4,7},{5,6},{6,5},{7,4},{8,11},{9,10},{10,... | collective-permute-start | bytes 1544 | tf_op jit(solution)/shard_map/ppermute | solution.py:258
  17.5 1.4 %shard_map.61 = f32[192,1024]{1,0:T(8,128)} custom-call(bf16[192,1024]{1,0:T(8,128)(2,1)S(1)} %get-tuple-element.18.refs_0_, bf16[192,1024]{1,0:T(8,128)(2,1)S(1)} %collective-permute-done.1.refs_1_, f32[192,192]{1,0:T(8,128)S(1)} %get-tuple-element.17.refs_7_.refs_2_, f32[192,192]{1,0:T(8,128)S(1)} %get-tuple-element.25.refs_3_, ...), custom_call_target="tpu_custom_call" | custom-call | flops 603979776 | bytes 1 | tf_op jit(solution)/shard_map/pallas_call | solution.py:169
  18.9 0.3 %collective-permute-done.7 = f32[1,128]{1,0:T(1,128)S(1)} collective-permute-done((f32[1,128]{1,0:T(1,128)S(1)}, f32[1,128]{1,0:T(1,128)S(1)}, u32[]{:S(2)}, u32[]{:S(2)}) %collective-permute-start.7) | collective-permute-done | bytes 544 | tf_op jit(solution)/shard_map/ppermute | solution.py:258
  19.2 0.5 %add.19 = f32[1,128]{1,0:T(1,128)} add(f32[1,128]{1,0:T(1,128)S(1)} %add_add_fusion, f32[1,128]{1,0:T(1,128)S(1)} %collective-permute-done.7) | non-fusion elementwise | flops 128 | bytes 1536 | tf_op jit(solution)/shard_map/add | solution.py:259
  (2 shorter events, 0.0 us)
Async XLA Ops:
  0.6 0.7 %copy-start = (s32[1,192]{1,0:T(1,128)S(1)}, s32[1,192]{1,0:T(1,128)}, u32[]{:S(2)}) copy-start(s32[1,192]{1,0:T(1,128)} %refs_2_.1) | copy-start | bytes 2308
  0.6 2.7 %collective-permute-start.1 = (bf16[192,1024]{1,0:T(8,128)(2,1)}, bf16[192,1024]{1,0:T(8,128)(2,1)S(1)}, u32[]{:S(2)}, u32[]{:S(2)}) collective-permute-start(bf16[192,1024]{1,0:T(8,128)(2,1)} %bitcast.7), channel_id=1, source_target_pairs={{0,1},{1,0},{2,3},{3,2},{4,5},{5,4},{6,7},{7,6},{8,9},{9,8},{10,11... | collective-permute-start | bytes 1179656 | tf_op jit(solution)/shard_map/ppermute | solution.py:197
  1.2 2.1 %collective-permute-start = (bf16[192,1024]{1,0:T(8,128)(2,1)}, bf16[192,1024]{1,0:T(8,128)(2,1)S(1)}, u32[]{:S(2)}, u32[]{:S(2)}) collective-permute-start(bf16[192,1024]{1,0:T(8,128)(2,1)} %bitcast.9), channel_id=1, source_target_pairs={{0,1},{1,0},{2,3},{3,2},{4,5},{5,4},{6,7},{7,6},{8,9},{9,8},{10,11... | collective-permute-start | bytes 1179656 | tf_op jit(solution)/shard_map/ppermute | solution.py:197
  1.3 2.0 %collective-permute-start.2 = (s32[1,192]{1,0:T(1,128)S(1)}, s32[1,192]{1,0:T(1,128)S(1)}, u32[]{:S(2)}, u32[]{:S(2)}) collective-permute-start(s32[1,192]{1,0:T(1,128)S(1)} %copy-done), channel_id=1, source_target_pairs={{0,1},{1,0},{2,3},{3,2},{4,5},{5,4},{6,7},{7,6},{8,9},{9,8},{10,11... | collective-permute-start | bytes 2312 | tf_op jit(solution)/shard_map/ppermute | solution.py:197
  4.4 6.0 %collective-permute-start.3 = (f32[1,128]{1,0:T(1,128)S(1)}, f32[1,128]{1,0:T(1,128)S(1)}, u32[]{:S(2)}, u32[]{:S(2)}) collective-permute-start(f32[1,128]{1,0:T(1,128)S(1)} %get-tuple-element.28), channel_id=1, source_target_pairs={{0,25},{1,24},{2,27},{3,26},{4,29},{5,28},{6,31},{7,30},{8,17},{9,... | collective-permute-start | bytes 1544 | tf_op jit(solution)/shard_map/ppermute | solution.py:258
  10.4 4.4 %collective-permute-start.6 = (f32[1,128]{1,0:T(1,128)S(1)}, f32[1,128]{1,0:T(1,128)S(1)}, u32[]{:S(2)}, u32[]{:S(2)}) collective-permute-start(f32[1,128]{1,0:T(1,128)S(1)} %add.15), channel_id=1, source_target_pairs={{0,9},{1,8},{2,11},{3,10},{4,13},{5,12},{6,15},{7,14},{8,1},{9,0},... | collective-permute-start | bytes 1544 | tf_op jit(solution)/shard_map/ppermute | solution.py:258
  10.4 4.4 %collective-permute-start.5 = (f32[1,128]{1,0:T(1,128)S(1)}, f32[1,128]{1,0:T(1,128)S(1)}, u32[]{:S(2)}, u32[]{:S(2)}) collective-permute-start(f32[1,128]{1,0:T(1,128)S(1)} %add.15), channel_id=1, source_target_pairs={{0,13},{1,12},{2,15},{3,14},{4,9},{5,8},{6,11},{7,10},{8,5},{9,4},... | collective-permute-start | bytes 1544 | tf_op jit(solution)/shard_map/ppermute | solution.py:258
  13.2 3.0 %collective-permute-start.4 = (f32[1,128]{1,0:T(1,128)S(1)}, f32[1,128]{1,0:T(1,128)S(1)}, u32[]{:S(2)}, u32[]{:S(2)}) collective-permute-start(f32[1,128]{1,0:T(1,128)S(1)} %add.15), channel_id=1, source_target_pairs={{0,5},{1,4},{2,7},{3,6},{4,1},{5,0},{6,3},{7,2},{8,13},{9,12},{10,... | collective-permute-start | bytes 1544 | tf_op jit(solution)/shard_map/ppermute | solution.py:258
  16.2 3.0 %collective-permute-start.7 = (f32[1,128]{1,0:T(1,128)S(1)}, f32[1,128]{1,0:T(1,128)S(1)}, u32[]{:S(2)}, u32[]{:S(2)}) collective-permute-start(f32[1,128]{1,0:T(1,128)S(1)} %add_add_fusion), channel_id=1, source_target_pairs={{0,3},{1,2},{2,1},{3,0},{4,7},{5,6},{6,5},{7,4},{8,11},{9,10},{10,... | collective-permute-start | bytes 1544 | tf_op jit(solution)/shard_map/ppermute | solution.py:258
